TPU v7x, 128 devices: a whole 4x4x4 slice. The times are simulated.
128 devices in a mesh: keys: 32 (over y, z, core), view: 4 (over x).
Axes of the slice: x: 4, y: 4, z: 4, core: 2. Of those that a mesh axis runs over, the one named last changes fastest.
Arguments:
- key_slot: int32 [16384], replicated, may hold values from 0 to 16383, as said below
- a_slot: int32 [524288], P(('keys', 'view')), may hold values from 0 to 511
- a_group: int32 [524288], P(('keys', 'view')), may hold values from 0 to 4095
- a_weight: int32 [524288], P(('keys', 'view')), may hold values from 1 to 3
- a_payload: bfloat16 [524288, 256], P(('keys', 'view')), may hold values from -1.1953125 to 1.1953125
- b_slot: int32 [524288], P(('keys', 'view')), may hold values from 0 to 511
- b_weight: int32 [524288], P(('keys', 'view')), may hold values from 1 to 3
- b_payload: bfloat16 [524288, 256], P(('keys', 'view')), may hold values from -0.59765625 to 0.59765625
- da_key: int32 [131072], P(('keys', 'view')), may hold values from 0 to 16383, as said below
- da_group: int32 [131072], P(('keys', 'view')), may hold values from 0 to 4095
- da_mult: int32 [131072], P(('keys', 'view')), may hold values from -1 to 1, as said below
- da_payload: bfloat16 [131072, 256], P(('keys', 'view')), may hold values from -1.796875 to 1.796875
- da_count: int32 [128], P(('keys', 'view')), may hold values from 768 to 1024, as said below
- db_key: int32 [131072], P(('keys', 'view')), may hold values from 0 to 16383, as said below
- db_mult: int32 [131072], P(('keys', 'view')), may hold values from -1 to 1, as said below
- db_payload: bfloat16 [131072, 256], P(('keys', 'view')), may hold values from -1.1953125 to 1.1953125
- db_count: int32 [128], P(('keys', 'view')), may hold values from 768 to 1024, as said below
Outputs:
- view_delta: float32 [4096, 256], P(('keys', 'view'))
Inputs may be any that keep to these rules, and one draw needn't show every extreme that they name: `key_slot`: A permutation of 0 to 16383. `da_key`: among the 1024 slots of one device, at most 64 have keys held by one keys index; in every draw one keys index gets exactly 64 live rows from every device. `db_key`: among the 1024 slots of one device, at most 64 have keys held by one keys index; in every draw one keys index gets exactly 64 live rows from every device. `da_mult`: each entry is -1 or 1. `db_mult`: each entry is -1 or 1. `da_count`: some device has all 1024 rows live. `db_count`: some device has all 1024 rows live.
All inputs are finite; a program needn't handle non-finite values.
Results may differ from a plain program's by a relative error of at most 0.0029.
Values may be sent and summed in bfloat16 or wider, within the bound.
A program may use at most 64 MiB of HBM per device.

v0:
```python
import jax
import jax.numpy as jnp
from jax import lax
from jax.sharding import Mesh
from jax.sharding import PartitionSpec as P

KEYS_DEV = 512
GROUPS_DEV = 32
DELTA_DEV = 1024
KEYS = ("keys_0", "keys_1", "keys_2")
KEYS_VIEW = ("keys_0", "keys_1", "keys_2", "view")


def sent_to_all(shard, axis):
    size = lax.axis_size(axis)
    return lax.all_to_all(
        jnp.broadcast_to(shard[None], (size, *shard.shape)), axis, 0, 0, tiled=True
    )


def of_everyone(shard, axis):
    return sent_to_all(shard, axis).sum(axis=0)


def together(arrays, axis):
    vector, at, gathered = (jnp.concatenate([a.reshape(-1) for a in arrays]), 0, [])
    so_far = of_everyone(vector, axis)
    for a in arrays:
        gathered.append(so_far[at : at + a.size].reshape(a.shape))
        at += a.size
    return tuple(gathered)


def own_block(blocks, axes, order):
    inside = blocks.shape[1:]
    blocks = blocks.reshape(*(lax.axis_size(a) for a in axes), *inside)
    blocks = jnp.moveaxis(blocks, order, range(len(axes))).reshape(-1, *inside)
    for k in order:
        blocks = lax.psum_scatter(blocks, axes[k], scatter_dimension=0, tiled=True)
    return blocks[0]


def in_blocks(shard, dim, size):
    dims = shard.shape
    blocks = shard.reshape(*dims[:dim], size, dims[dim] // size, *dims[dim + 1 :])
    return jnp.moveaxis(blocks, dim, 0)


def sum_by_axis(shard, axes, order, dim):
    size = lax.axis_size(axes)
    return own_block(in_blocks(shard, dim, size), axes, order)


def pack_rows(key_slot, row_keys, row_mult, row_count, payload, extra_columns, owners):
    capacity = 2 * DELTA_DEV // owners
    alive_rows = jnp.arange(DELTA_DEV, dtype=jnp.int32) < row_count[0]
    slots = jnp.take(key_slot, row_keys)
    target = slots // KEYS_DEV
    marks = (target[:, None] == jnp.arange(owners, dtype=jnp.int32)[None, :]).astype(
        jnp.int32
    ) * alive_rows[:, None].astype(jnp.int32)
    before = jnp.cumsum(marks, axis=0) - marks
    slot_rank = jnp.take_along_axis(before, target[:, None], axis=1)[:, 0]
    position = jnp.where(alive_rows, target * capacity + slot_rank, owners * capacity)
    columns = jnp.stack(
        [slots % KEYS_DEV, row_mult * alive_rows.astype(jnp.int32)] + extra_columns, axis=1
    )
    sent_payload = (
        jnp.zeros((owners * capacity + 1, payload.shape[1]), payload.dtype)
        .at[position]
        .set(payload)
    )
    sent_columns = (
        jnp.zeros((owners * capacity + 1, columns.shape[1]), jnp.int32).at[position].set(columns)
    )
    return (
        sent_payload[:-1].reshape(owners, capacity, payload.shape[1]),
        sent_columns[:-1].reshape(owners, capacity, columns.shape[1]),
    )


def shards(
    key_slot,
    a_slot,
    a_group,
    a_weight,
    a_payload,
    b_slot,
    b_weight,
    b_payload,
    da_key,
    da_group,
    da_mult,
    da_payload,
    da_count,
    db_key,
    db_mult,
    db_payload,
    db_count,
):
    owners = lax.axis_size(KEYS)
    width = a_payload.shape[1]
    a_sent, a_columns = pack_rows(
        key_slot, da_key, da_mult, da_count, da_payload, [da_group], owners
    )
    a_payload_in, a_columns_in = (
        lax.all_to_all(a_sent, KEYS, split_axis=0, concat_axis=0, tiled=True),
        lax.all_to_all(a_columns, KEYS, split_axis=0, concat_axis=0, tiled=True),
    )
    weighted_b = b_weight[:, None].astype(jnp.float32) * b_payload.astype(jnp.float32)
    local_b = jax.ops.segment_sum(weighted_b, b_slot, num_segments=KEYS_DEV)
    b_sent, b_columns = pack_rows(key_slot, db_key, db_mult, db_count, db_payload, [], owners)
    b_payload_in, b_columns_in = (
        lax.all_to_all(b_sent, KEYS, split_axis=0, concat_axis=0, tiled=True),
        lax.all_to_all(b_columns, KEYS, split_axis=0, concat_axis=0, tiled=True),
    )
    flat_columns = b_columns_in.reshape(-1, 2)
    terms = flat_columns[:, 1:2].astype(jnp.float32) * b_payload_in.reshape(-1, width).astype(
        jnp.float32
    )
    local_db = jax.ops.segment_sum(terms, flat_columns[:, 0], num_segments=KEYS_DEV)
    total_b, total_db = together((local_b, local_db), "view")
    whole_table = total_b + total_db
    a_terms = (
        a_weight[:, None].astype(jnp.float32)
        * a_payload.astype(jnp.float32)
        * jnp.take(total_db, a_slot, axis=0)
    ).astype(jnp.bfloat16)
    delta_columns = a_columns_in.reshape(-1, 3)
    delta_terms = (
        delta_columns[:, 1:2].astype(jnp.float32)
        * a_payload_in.reshape(-1, width).astype(jnp.float32)
        * jnp.take(whole_table, delta_columns[:, 0], axis=0)
    ).astype(jnp.bfloat16)
    all_terms = jnp.concatenate([a_terms, delta_terms], axis=0)
    all_groups = jnp.concatenate([a_group, delta_columns[:, 2]])
    row_total = GROUPS_DEV * lax.axis_size(KEYS_VIEW)
    shifted = all_groups - jnp.int32(0)
    inside = (shifted >= 0) & (shifted < row_total)
    segment_index = jnp.where(inside, shifted, row_total)
    summed = jax.ops.segment_sum(
        all_terms.astype(jnp.float32), segment_index, num_segments=row_total + 1
    )
    return sum_by_axis(summed[:row_total], KEYS_VIEW, (2, 0, 1, 3), 0)


def solution(mesh):
    split = Mesh(
        mesh.devices.reshape(4, 4, 2, mesh.shape["view"]), ("keys_0", "keys_1", "keys_2", "view")
    )
    placed = (
        P(),
        P(KEYS_VIEW),
        P(KEYS_VIEW),
        P(KEYS_VIEW),
        P(KEYS_VIEW, None),
        P(KEYS_VIEW),
        P(KEYS_VIEW),
        P(KEYS_VIEW, None),
        P(KEYS_VIEW),
        P(KEYS_VIEW),
        P(KEYS_VIEW),
        P(KEYS_VIEW, None),
        P(KEYS_VIEW),
        P(KEYS_VIEW),
        P(KEYS_VIEW),
        P(KEYS_VIEW, None),
        P(KEYS_VIEW),
    )
    return jax.shard_map(
        shards, mesh=split, in_specs=placed, out_specs=P(KEYS_VIEW, None), check_vma=False
    )
```

profile of v0, /device:TPU:1, one launch (start us, length us, event | category | flops | bytes accessed | tf_op | source)
XLA Modules:
  0.0 391.3 jit_solution(4001793434923842289)
XLA Ops:
  6.5 0.7 fusion.48
  7.4 6.1 %gather_fusion.4 = s32[1024]{0:T(1024)S(1)} fusion(s32[16384]{0:T(1024)S(1)} %copy-done, s32[1024]{0:T(1024)S(1)} %fusion.48), kind=kCustom, calls=%fused_computation.2.clone | custom fusion | bytes 12288 | tf_op jit(solution)/shard_map/jit(_take)/gather | solution.py:57
  14.2 9.0 %reduce-window.16 = s32[32,8,128]{2,1,0:T(8,128)S(1)} reduce-window(s32[32,8,128]{2,1,0:T(8,128)S(1)} %fusion.27, s32[]{:T(128)} %constant.102.clone.1), window={size=1x1x128 pad=0_0x0_0x127_0}, to_apply=%region_4.7 | reduce-window | flops 4161536 | bytes 262148 | tf_op jit(solution)/shard_map/reduce-window.2
  23.7 6.2 %gather_fusion.2 = s32[1024]{0:T(1024)S(1)} fusion(s32[16384]{0:T(1024)S(1)} %copy-done, s32[1024]{0:T(1024)S(1)} %fusion.47), kind=kCustom, calls=%fused_computation.clone | custom fusion | bytes 12288 | tf_op jit(solution)/shard_map/jit(_take)/gather | solution.py:57
  30.1 8.6 %gather_fusion.5 = s32[1024]{0:T(1024)S(1)} fusion(s32[1024,32]{0,1:T(8,128)S(1)} %fusion.24, s32[1024]{0:T(1024)S(1)} %bitcast.84), kind=kCustom, calls=%fused_computation.3.clone | custom fusion | bytes 16384 | tf_op jit(solution)/shard_map/jit(take_along_axis)/gather | solution.py:63
  38.8 0.2 copy.70
  39.0 3.3 scatter_custom_fusion.2
  42.4 0.4 copy.71
  42.8 0.7 reshape.388
  43.5 9.6 %all-to-all-start.1 = ((s32[32,1,128]{2,1,0:T(1,128)}), s32[32,1,128]{2,1,0:T(1,128)S(1)}, u32[]{:S(2)}, u32[]{:S(2)}) async-start(s32[32,1,128]{2,1,0:T(1,128)} %reshape.388), calls=%async_computation.1 | async-start | bytes 32768 | tf_op jit(solution)/shard_map/all_to_all | solution.py:115
  53.8 9.0 %reduce-window.14 = s32[32,8,128]{2,1,0:T(8,128)S(1)} reduce-window(s32[32,8,128]{2,1,0:T(8,128)S(1)} %fusion.26, s32[]{:T(128)} %constant.102.clone.1), window={size=1x1x128 pad=0_0x0_0x127_0}, to_apply=%region_0.0 | reduce-window | flops 4161536 | bytes 262148 | tf_op jit(solution)/shard_map/reduce-window
  63.3 5.6 %scatter_custom_fusion.3 = bf16[2049,256]{1,0:T(8,128)(2,1)S(1)} fusion(s32[1024]{0:T(1024)S(1)} %get-tuple-element.23, bf16[1024,256]{1,0:T(8,128)(2,1)} %param.36, bf16[]{:T(256)} %constant.113.clone.1), kind=kCustom, calls=%fused_computation.33 | custom fusion | bytes 1049600 | tf_op jit(solution)/shard_map/scatter | solution.py:71
  69.0 1.1 slice.115
  70.1 7.4 %all-to-all-start.2 = ((bf16[32,64,256]{2,1,0:T(8,128)(2,1)}), bf16[32,64,256]{2,1,0:T(8,128)(2,1)S(1)}, u32[]{:S(2)}, u32[]{:S(2)}) async-start(bf16[32,64,256]{2,1,0:T(8,128)(2,1)} %bitcast.31), calls=%async_computation.2 | async-start | bytes 2097152 | tf_op jit(solution)/shard_map/all_to_all | solution.py:114
  77.5 25.2 %scatter_custom_fusion.1 = f32[512,256]{1,0:T(8,128)S(1)} fusion(s32[4096]{0:T(1024)} %param.26, bf16[4096,256]{1,0:T(8,128)(2,1)} %param.28, f32[4096]{0:T(1024)S(1)} %convert_element_type.71, f32[]{:T(128)} %constant.101.clone.1), kind=kCustom, calls=%fused_computation.16 | custom fusion | flops 3145728 | bytes 2638336 | tf_op jit(solution)/shard_map/scatter-add | solution.py:111
  102.7 1.1 copy.79
  103.8 8.6 %gather_fusion.3 = s32[1024]{0:T(1024)S(1)} fusion(s32[1024,32]{0,1:T(8,128)S(1)} %fusion.25, s32[1024]{0:T(1024)S(1)} %bitcast.83), kind=kCustom, calls=%fused_computation.1.clone | custom fusion | bytes 16384 | tf_op jit(solution)/shard_map/jit(take_along_axis)/gather | solution.py:63
  112.5 0.2 copy.65
  112.7 3.3 scatter_custom_fusion
  116.1 0.4 copy.66
  116.5 0.7 reshape.386
  117.2 0.6 broadcast.221
  117.8 0.7 reduce.4
  118.7 7.4 %all-to-all-start = ((s32[32,1,192]{2,1,0:T(1,128)}), s32[32,1,192]{2,1,0:T(1,128)S(1)}, u32[]{:S(2)}, u32[]{:S(2)}) async-start(s32[32,1,192]{2,1,0:T(1,128)} %reshape.386), calls=%async_computation | async-start | bytes 65536 | tf_op jit(solution)/shard_map/all_to_all | solution.py:108
  126.1 13.8 %scatter_custom_fusion.4 = f32[512,256]{1,0:T(8,128)S(1)} fusion(s32[2048]{0:T(1024)S(1)} %bitcast.121, bf16[2048,256]{1,0:T(8,128)(2,1)S(1)} %bitcast.87, f32[2048]{0:T(1024)S(1)} %bitcast.107, f32[]{:T(128)} %constant.101.clone.1), kind=kCustom, calls=%fused_computation.27 | custom fusion | flops 1572864 | bytes 1581060 | tf_op jit(solution)/shard_map/scatter-add | solution.py:121
  139.9 0.3 copy.81
  140.2 1.1 pad_maximum_fusion
  141.3 4.6 %broadcast_in_dim.89 = f32[4,1,262144]{2,1,0:T(1,128)} broadcast(f32[262144]{0:T(1024)S(1)} %pad_maximum_fusion), dimensions={2} | broadcast | bytes 5242880 | tf_op jit(solution)/shard_map/broadcast_in_dim | solution.py:17
  145.9 5.0 %all-to-all-start.3 = ((f32[4,1,262144]{2,1,0:T(1,128)}), f32[4,1,262144]{2,1,0:T(1,128)}, u32[]{:S(2)}, u32[]{:S(2)}) async-start(f32[4,1,262144]{2,1,0:T(1,128)} %broadcast_in_dim.89), calls=%async_computation.3 | async-start | bytes 8388608 | tf_op jit(solution)/shard_map/all_to_all | solution.py:16
  151.0 5.6 %scatter_custom_fusion.5 = bf16[2049,256]{1,0:T(8,128)(2,1)S(1)} fusion(s32[1024]{0:T(1024)S(1)} %get-tuple-element.21, bf16[1024,256]{1,0:T(8,128)(2,1)} %param.32, bf16[]{:T(256)} %constant.113.clone.1), kind=kCustom, calls=%fused_computation.31 | custom fusion | bytes 1049600 | tf_op jit(solution)/shard_map/scatter | solution.py:71
  156.6 1.1 slice.118
  157.8 0.7 reduce.3
  158.9 40.8 %all-to-all-done.3 = f32[4,1,262144]{2,1,0:T(1,128)} async-done(((f32[4,1,262144]{2,1,0:T(1,128)}), f32[4,1,262144]{2,1,0:T(1,128)}, u32[]{:S(2)}, u32[]{:S(2)}) %all-to-all-start.3) | async-done | bytes 4194336 | tf_op jit(solution)/shard_map/all_to_all | solution.py:16
  199.7 7.8 %all-to-all-start.4 = ((bf16[32,64,256]{2,1,0:T(8,128)(2,1)}), bf16[32,64,256]{2,1,0:T(8,128)(2,1)}, u32[]{:S(2)}, u32[]{:S(2)}) async-start(bf16[32,64,256]{2,1,0:T(8,128)(2,1)} %bitcast.34), calls=%async_computation.4 | async-start | bytes 2097152 | tf_op jit(solution)/shard_map/all_to_all | solution.py:107
  207.5 0.3 reduce-scatter.5.cloned.1.call-start
  207.8 9.8 %reduce_sum.9 = f32[262144]{0:T(1024)S(1)} reduce(f32[4,1,262144]{2,1,0:T(1,128)} %all-to-all-done.3, f32[]{:T(128)} %constant.101.clone.1), dimensions={0,1}, to_apply=%region_9.12 | reduce | flops 786432 | bytes 5242884 | tf_op jit(solution)/shard_map/reduce_sum | solution.py:22
  217.7 0.1 slice.79
  218.0 16.1 %gather_fusion = f32[4096,256]{1,0:T(8,128)} fusion(f32[512,256]{1,0:T(8,128)S(1)} %slice.79, s32[4096]{0:T(1024)S(1)} %fusion.28), kind=kCustom, calls=%fused_computation.4 | custom fusion | bytes 8404992 | tf_op jit(solution)/shard_map/jit(_take)/gather | solution.py:127
  234.2 6.6 %gather_fusion.1 = f32[2048,256]{1,0:T(8,128)S(1)} fusion(f32[512,256]{1,0:T(8,128)S(1)} %add.85, s32[2048]{0:T(1024)S(1)} %broadcast_clamp_fusion), kind=kCustom, calls=%fused_computation.5 | custom fusion | bytes 4202496 | tf_op jit(solution)/shard_map/jit(_take)/gather | solution.py:133
  240.8 5.9 %multiply_convert_fusion = bf16[4096,256]{1,0:T(8,128)(2,1)} fusion(f32[4096,256]{1,0:T(8,128)} %gather_fusion, bf16[4096,256]{1,0:T(8,128)(2,1)} %param.25, f32[4096]{0:T(1024)S(1)} %convert_element_type.69, pred[4096]{0:T(1024)(128)(4,1)S(1)} %compare_and_fusion), kind=kLoop, calls=%fused_computation.15 | loop fusion | flops 5242880 | bytes 8409088 | tf_op jit(solution)/shard_map/convert_element_type | solution.py:128
  246.7 1.8 fusion.10
  248.4 40.1 %scatter_custom_fusion.6 = f32[4097,256]{1,0:T(8,128)} fusion(s32[6144]{0:T(1024)S(1)} %bitcast.109, bf16[2048,256]{1,0:T(8,128)(2,1)S(1)} %fusion.10, bf16[]{:T(256)} %constant.156, bf16[4096,256]{1,0:T(8,128)(2,1)} %multiply_convert_fusion, f32[]{:T(128)} %constant.101.clone.1), kind=kCustom, calls=%fused_computation.13 | custom fusion | flops 7864320 | bytes 7341062 | tf_op jit(solution)/shard_map/scatter-add | solution.py:141
  288.6 2.2 slice-done
  290.8 2.2 copy.74
  293.1 14.3 %reduce-scatter.5.cloned.1.call-done = f32[64,32,256]{2,1,0:T(8,128)} async-done(((f32[128,32,256]{2,1,0:T(8,128)}), f32[64,32,256]{2,1,0:T(8,128)}) %reduce-scatter.5.cloned.1.call-update) | async-done | bytes 2097168 | tf_op jit(solution)/shard_map/reduce_scatter | solution.py:39
  307.5 33.1 %reduce-scatter.7.cloned.1.call-done = f32[16,32,256]{2,1,0:T(8,128)} async-done(((f32[64,32,256]{2,1,0:T(8,128)}), f32[16,32,256]{2,1,0:T(8,128)}) %reduce-scatter.7.cloned.1.call-update) | async-done | bytes 524304 | tf_op jit(solution)/shard_map/reduce_scatter | solution.py:39
  340.6 21.7 %reduce-scatter.9.cloned.1.call-done = f32[4,32,256]{2,1,0:T(8,128)} async-done(((f32[16,32,256]{2,1,0:T(8,128)}), f32[4,32,256]{2,1,0:T(8,128)}) %reduce-scatter.9.cloned.1.call-update) | async-done | bytes 131088 | tf_op jit(solution)/shard_map/reduce_scatter | solution.py:39
  362.3 22.4 %reduce-scatter.11.cloned.1.call-done = f32[1,32,256]{2,1,0:T(8,128)} async-done(((f32[4,32,256]{2,1,0:T(8,128)}), f32[1,32,256]{2,1,0:T(8,128)}) %reduce-scatter.11.cloned.1.call-update) | async-done | bytes 32784 | tf_op jit(solution)/shard_map/reduce_scatter | solution.py:39
  (87 shorter events, 2.4 us)
Async XLA Ops:
  6.5 0.8 copy-start
  7.4 6.2 %copy-start.5 = (s32[1024]{0:T(1024)S(1)}, s32[1024]{0:T(1024)}, u32[]{:S(2)}) copy-start(s32[1024]{0:T(1024)} %param.34) | copy-start | bytes 12292
  7.4 16.3 %copy-start.6 = (s32[1024]{0:T(1024)S(1)}, s32[1024]{0:T(1024)}, u32[]{:S(2)}) copy-start(s32[1024]{0:T(1024)} %param.29) | copy-start | bytes 12292
  30.1 8.7 %copy-start.8 = (s32[1024]{0:T(1024)S(1)}, s32[1024]{0:T(1024)}, u32[]{:S(2)}) copy-start(s32[1024]{0:T(1024)} %param.35) | copy-start | bytes 12292
  43.5 26.5 %all-to-all-start.1 = ((s32[32,1,128]{2,1,0:T(1,128)}), s32[32,1,128]{2,1,0:T(1,128)S(1)}, u32[]{:S(2)}, u32[]{:S(2)}) async-start(s32[32,1,128]{2,1,0:T(1,128)} %reshape.388), calls=%async_computation.1 | async-start | bytes 32768 | tf_op jit(solution)/shard_map/all_to_all | solution.py:115
  69.0 8.5 %copy-start.3 = (s32[4096]{0:T(1024)S(1)}, s32[4096]{0:T(1024)}, u32[]{:S(2)}) copy-start(s32[4096]{0:T(1024)} %param.27) | copy-start | bytes 49156
  70.1 48.6 %all-to-all-start.2 = ((bf16[32,64,256]{2,1,0:T(8,128)(2,1)}), bf16[32,64,256]{2,1,0:T(8,128)(2,1)S(1)}, u32[]{:S(2)}, u32[]{:S(2)}) async-start(bf16[32,64,256]{2,1,0:T(8,128)(2,1)} %bitcast.31), calls=%async_computation.2 | async-start | bytes 2097152 | tf_op jit(solution)/shard_map/all_to_all | solution.py:114
  103.8 8.7 %copy-start.9 = (s32[1024]{0:T(1024)S(1)}, s32[1024]{0:T(1024)}, u32[]{:S(2)}) copy-start(s32[1024]{0:T(1024)} %param.31) | copy-start | bytes 12292
  103.8 8.7 %copy-start.7 = (s32[1024]{0:T(1024)S(1)}, s32[1024]{0:T(1024)}, u32[]{:S(2)}) copy-start(s32[1024]{0:T(1024)} %param.30) | copy-start | bytes 12292
  118.7 22.6 %all-to-all-start = ((s32[32,1,192]{2,1,0:T(1,128)}), s32[32,1,192]{2,1,0:T(1,128)S(1)}, u32[]{:S(2)}, u32[]{:S(2)}) async-start(s32[32,1,192]{2,1,0:T(1,128)} %reshape.386), calls=%async_computation | async-start | bytes 65536 | tf_op jit(solution)/shard_map/all_to_all | solution.py:108
  145.9 5.0 %copy-start.4 = (s32[4096]{0:T(1024)S(1)}, s32[4096]{0:T(1024)}, u32[]{:S(2)}) copy-start(s32[4096]{0:T(1024)} %param.24) | copy-start | bytes 49156
  145.9 53.7 %all-to-all-start.3 = ((f32[4,1,262144]{2,1,0:T(1,128)}), f32[4,1,262144]{2,1,0:T(1,128)}, u32[]{:S(2)}, u32[]{:S(2)}) async-start(f32[4,1,262144]{2,1,0:T(1,128)} %broadcast_in_dim.89), calls=%async_computation.3 | async-start | bytes 8388608 | tf_op jit(solution)/shard_map/all_to_all | solution.py:16
  151.0 6.8 %copy-start.1 = (s32[4096]{0:T(1024)S(1)}, s32[4096]{0:T(1024)}, u32[]{:S(2)}) copy-start(s32[4096]{0:T(1024)} %param.22) | copy-start | bytes 49156
  151.0 7.8 %copy-start.2 = (s32[4096]{0:T(1024)S(1)}, s32[4096]{0:T(1024)}, u32[]{:S(2)}) copy-start(s32[4096]{0:T(1024)} %param.23) | copy-start | bytes 49156
  199.7 47.0 %all-to-all-start.4 = ((bf16[32,64,256]{2,1,0:T(8,128)(2,1)}), bf16[32,64,256]{2,1,0:T(8,128)(2,1)}, u32[]{:S(2)}, u32[]{:S(2)}) async-start(bf16[32,64,256]{2,1,0:T(8,128)(2,1)} %bitcast.34), calls=%async_computation.4 | async-start | bytes 2097152 | tf_op jit(solution)/shard_map/all_to_all | solution.py:107
  207.5 99.9 %reduce-scatter.5.cloned.1.call-start = ((), (), s32[]{:S(2)}) async-start(), calls=%async_computation.9 | async-start | bytes 6291456 | tf_op jit(solution)/shard_map/reduce_scatter | solution.py:39
  288.6 2.2 slice-start
  293.0 47.5 %reduce-scatter.7.cloned.1.call-start = ((), (), s32[]{:S(2)}) async-start(), calls=%async_computation.10 | async-start | bytes 2621440 | tf_op jit(solution)/shard_map/reduce_scatter | solution.py:39
  307.4 54.9 %reduce-scatter.9.cloned.1.call-start = ((), (), s32[]{:S(2)}) async-start(), calls=%async_computation.11 | async-start | bytes 655360 | tf_op jit(solution)/shard_map/reduce_scatter | solution.py:39
  340.6 44.1 %reduce-scatter.11.cloned.1.call-start = ((), (), s32[]{:S(2)}) async-start(), calls=%async_computation.12 | async-start | bytes 163840 | tf_op jit(solution)/shard_map/reduce_scatter | solution.py:39
Sparse Core Ops, SparseCore 0:
  293.2 14.1 reduce-scatter.4
  309.8 30.7 reduce-scatter.6
  342.9 19.2 reduce-scatter.8
  364.5 20.1 reduce-scatter.10
where the time goes:
time: 394 us; the launch traced here: 391 us
  waiting for transfers between devices  132 us (34%)
  other arithmetic  119 us (30%)
  local copies, waits for them, and re-layouts  87.7 us (22%)
  starting transfers between devices  37.6 us (10%)
  between operations  15.1 us (4%)
    reduce_scatter x4, waiting for transfers between devices, own_block(): blocks = lax.psum_scatter(blocks, axes[k], scatter_dimension=0, tiled=True)  91.5 us
    all_to_all x1, waiting for transfers between devices, sent_to_all(): lax.all_to_all(jnp.broadcast_to(shard[None], (size, *shard.shape)), axis,...  40.8 us
    scatter-add x1, other arithmetic, shards(): jax.ops.segment_sum(all_terms.astype(jnp.float32), segment_index, num_seg...  40.1 us
    scatter-add x1, other arithmetic, shards(): local_b = jax.ops.segment_sum(weighted_b, b_slot, num_segments=KEYS_DEV)  25.2 us
    another operation x6, other arithmetic  18.3 us
    gather x2, local copies, waits for them, and re-layouts, pack_rows(): slot_rank = jnp.take_along_axis(before, target[:, None], axis=1)[:, 0]  17.3 us
    gather x1, local copies, waits for them, and re-layouts, shards(): jnp.take(total_db, a_slot, axis=0)  16.1 us
    scatter-add x1, other arithmetic, shards(): jax.ops.segment_sum(terms, flat_columns[:, 0], num_segments=KEYS_DEV)  13.8 us
  transfers between devices with their start and end apart: 9, of which 5 were waited for; matrix products, arithmetic and copies ran while one was open for 30% of the time, Pallas kernels for 0%

commit v1 on v0

v1 whole, which is shorter than its diff:
```python
import functools

import jax
import jax.numpy as jnp
from jax import lax
from jax.experimental import pallas as pl
from jax.experimental.pallas import tpu as pltpu
from jax.sharding import PartitionSpec as P

MESH = pl.DeviceIdType.MESH
F32, BF16, I32 = jnp.float32, jnp.bfloat16, jnp.int32
D = 256
KEYS_DEV = 512
GROUPS_DEV = 32
ROWS = 4096
DELTA = 1024
CAP = 64
OWNERS = 32
VIEWS = 4
LANES = 128
PEERS = 64
HALF = 2048


def iota(shape, dim):
    return lax.broadcasted_iota(I32, shape, dim)


def dot(a, b):
    return jnp.dot(a, b, preferred_element_type=F32)


def one_hot(rows, height, base, values=None):
    at = iota((height, LANES), 0)
    parts = []
    for n, row in enumerate(rows):
        value = 1.0 if values is None else values[n]
        parts.append(jnp.where(at == row - base, value, 0.0).astype(BF16))
    return jnp.concatenate(parts, axis=1)


def split_rows(ref):
    return [ref[s : s + 1, :] for s in range(ref.shape[0])]


def places(table, key_ref, count):
    keys = split_rows(key_ref)
    at = iota((LANES, LANES), 0)
    hits = jnp.concatenate(
        [jnp.where(at == (k >> 7), 1.0, 0.0).astype(BF16) for k in keys], axis=1
    )
    found = dot(table, hits)
    slots, owners, lives, marks = [], [], [], []
    lane = iota((1, LANES), 1)
    owner_at = iota((OWNERS, LANES), 0)
    for s, k in enumerate(keys):
        cut = slice(s * LANES, (s + 1) * LANES)
        value = found[:LANES, cut] * 128.0 + found[LANES:, cut]
        slot = jnp.sum(jnp.where(at == (k & 127), value, 0.0), axis=0, keepdims=True).astype(I32)
        live = lane + s * LANES < count
        owner = jnp.where(live, slot >> 9, -1)
        slots.append(slot & (KEYS_DEV - 1))
        owners.append(owner)
        lives.append(live)
        marks.append(jnp.where(owner_at == owner, 1.0, 0.0))
    stacked = jnp.concatenate(marks, axis=0).astype(BF16)
    col = iota((LANES, 2 * LANES), 1)
    before = jnp.where((iota((LANES, 2 * LANES), 0) < col) | (col >= LANES), 1.0, 0.0).astype(BF16)
    counts = dot(stacked, before)
    carry = jnp.zeros((OWNERS, LANES), F32)
    spots = []
    for s in range(len(keys)):
        cut = slice(s * OWNERS, (s + 1) * OWNERS)
        rank = jnp.sum(marks[s] * (counts[cut, :LANES] + carry), axis=0, keepdims=True).astype(I32)
        spots.append(jnp.where(lives[s], owners[s] * CAP + rank, -1))
        carry = carry + counts[cut, LANES:]
    return slots, spots


def pack_kernel(
    key_slot, da_key, da_group, da_mult, db_key, db_mult, da_count, db_count, da_rows, db_rows,
    da_out, db_out, info_out, spot_ref, sign_ref, info_ref,
):
    whole = key_slot[...]
    high = (whole >> 7).astype(F32).T
    low = (whole & 127).astype(F32).T
    table = jnp.concatenate([high, low], axis=0).astype(BF16)
    for r, (key_ref, mult_ref, count_ref) in enumerate(
        ((db_key, db_mult, db_count), (da_key, da_mult, da_count))
    ):
        slots, spots = places(table, key_ref, count_ref[0])
        for s in range(8):
            cut = slice(s * LANES, (s + 1) * LANES)
            spot_ref[8 * r + s : 8 * r + s + 1, :] = spots[s]
            sign_ref[8 * r + s : 8 * r + s + 1, :] = mult_ref[s : s + 1, :].astype(F32)
            group = da_group[s : s + 1, :]
            rows = [slots[s] >> 4, slots[s] & 15, group >> 6, group & 63]
            zero = jnp.zeros((4, LANES), F32)
            info_ref[r, :, cut] = jnp.concatenate(
                [row.astype(F32) for row in rows] + [zero], axis=0
            ).astype(BF16)

    def chunk(c, carry):
        base = c * 256
        notes = []
        for r, (rows, out) in enumerate(((db_rows, db_out), (da_rows, da_out))):
            spots = [spot_ref[8 * r + s : 8 * r + s + 1, :] for s in range(8)]
            signs = [sign_ref[8 * r + s : 8 * r + s + 1, :] for s in range(8)]
            pick = one_hot(spots, 256, base, signs)
            out[pl.ds(pl.multiple_of(base, 256), 256), :] = dot(pick, rows[...]).astype(BF16)
            notes.append(
                jnp.abs(
                    lax.dot_general(
                        info_ref[r], pick, (((1,), (1,)), ((), ())), preferred_element_type=F32
                    )
                )
            )
        b, a = notes
        rows = jnp.concatenate(
            [
                b[0:1] * 16.0 + b[1:2],
                a[0:1] * 16.0 + a[1:2],
                a[2:3] * 64.0 + a[3:4],
                jnp.zeros((5, 256), F32),
            ],
            axis=0,
        )
        first = iota((8, LANES), 1) < CAP
        for j in range(4):
            v = rows[:, (j // 2) * LANES : (j // 2 + 1) * LANES]
            turned = pltpu.roll(v, CAP, 1)
            kept = jnp.where(first, v, turned) if j % 2 == 0 else jnp.where(first, turned, v)
            info_out[4 * c + j] = kept.astype(I32)
        return carry

    lax.fori_loop(0, 8, chunk, 0)


def wait_bytes(ref, sem):
    pltpu.make_async_copy(ref, ref, sem).wait()


def main_kernel(
    db_send, da_send, info_send, b_rows, b_slot, b_weight, a_rows, a_slot, a_weight, a_group,
    out, db_recv, da_recv, info_recv, part_b, part_db, quarter_b, quarter_db, got_b, got_db,
    full_b, full_db, pick, pick_d, table_hl, table_w, terms, spots, near_send, near_recv,
    far_send, far_recv, own, sems, near_sems,
):
    k, x = lax.axis_index("keys"), lax.axis_index("view")
    core = lax.rem(k, 2)
    partner = k + 1 - 2 * core
    seat = (k // 2) * VIEWS + x

    def peer(j):
        t = lax.rem(seat + j, PEERS)
        return {"keys": (t // VIEWS) * 2 + core, "view": lax.rem(t, VIEWS)}

    def send(src, dst, sem_s, sem_r, device):
        return pltpu.make_async_remote_copy(
            src_ref=src, dst_ref=dst, send_sem=sem_s, recv_sem=sem_r, device_id=device,
            device_id_type=MESH,
        )

    barrier = pltpu.get_barrier_semaphore()

    def greet_same(j, carry):
        pl.semaphore_signal(barrier, inc=1, device_id=peer(j), device_id_type=MESH)
        return carry

    def greet_other(j, carry):
        to = {"keys": lax.rem(k + 2 * j + 1, OWNERS), "view": x}
        pl.semaphore_signal(barrier, inc=1, device_id=to, device_id_type=MESH)
        return carry

    lax.fori_loop(1, PEERS, greet_same, 0)
    lax.fori_loop(0, OWNERS // 2, greet_other, 0)
    pl.semaphore_wait(barrier, PEERS - 1 + OWNERS // 2)

    def to_owner(j, carry):
        owner = lax.rem(k + j, OWNERS)
        to = {"keys": owner, "view": x}
        send(info_send.at[owner], info_recv.at[OWNERS - j], sems.at[0], sems.at[1], to).start()
        send(db_send.at[owner], db_recv.at[OWNERS - j], sems.at[2], sems.at[3], to).start()
        return carry

    lax.fori_loop(1, OWNERS, to_owner, 0)

    def to_owner_a(j, carry):
        owner = lax.rem(k + j, OWNERS)
        to = {"keys": owner, "view": x}
        send(da_send.at[owner], da_recv.at[OWNERS - j], sems.at[4], sems.at[5], to).start()
        return carry

    lax.fori_loop(1, OWNERS, to_owner_a, 0)
    info_recv[0] = info_send[k]
    db_recv[0] = db_send[k]
    da_recv[0] = da_send[k]

    for m in range(2):
        acc = jnp.zeros((256, D), F32)
        for p in range(8):
            rows = [b_slot[4 * p + s : 4 * p + s + 1, :] for s in range(4)]
            values = [b_weight[4 * p + s : 4 * p + s + 1, :].astype(F32) for s in range(4)]
            acc = acc + dot(one_hot(rows, 256, 256 * m, values), b_rows[512 * p : 512 * (p + 1), :])
        part_b[256 * m : 256 * (m + 1), :] = acc

    def quarter(at):
        return pl.ds(pl.multiple_of(at * 128, 128), 128)

    def across(part, got, s):
        for j in range(1, VIEWS):
            to = lax.rem(x + j, VIEWS)
            send(
                part.at[quarter(to)], got.at[j - 1], sems.at[s], sems.at[s + 1],
                {"keys": k, "view": to},
            ).start()

    def all_quarters(mine, full, s):
        for j in range(1, VIEWS):
            to = lax.rem(x + j, VIEWS)
            send(
                mine, full.at[quarter(x)], sems.at[s], sems.at[s + 1], {"keys": k, "view": to}
            ).start()

    across(part_b, got_b, 6)

    at_lane = iota((LANES, LANES), 1)

    def pick_block(j, carry):
        row = a_slot[pl.ds(j, 1), :] + KEYS_DEV * a_weight[pl.ds(j, 1), :]
        cols = jnp.broadcast_to(row.astype(F32), (LANES, LANES)).T.astype(I32)
        slot, weight = cols & (KEYS_DEV - 1), (cols >> 9).astype(F32)
        at = pl.ds(pl.multiple_of(j * LANES, LANES), LANES)
        for q in range(4):
            pick[at, q * LANES : (q + 1) * LANES] = jnp.where(
                at_lane + q * LANES == slot, weight, 0.0
            ).astype(BF16)
        return carry

    lax.fori_loop(0, 32, pick_block, 0)

    def place(group):
        device = group >> 5
        seat_g = (device >> 3) * VIEWS + (device & 3)
        other = ((device >> 2) & 1) ^ core
        return other * HALF + ((seat_g - seat) & (PEERS - 1)) * GROUPS_DEV + (group & 31)

    spots[0:32, :] = place(a_group[...])

    wait_bytes(got_b, sems.at[7])
    quarter_b[...] = part_b[quarter(x), :] + got_b[0] + got_b[1] + got_b[2]
    all_quarters(quarter_b, full_b, 8)
    full_b[quarter(x), :] = quarter_b[...]

    wait_bytes(info_recv.at[1:OWNERS], sems.at[1])
    left = iota((1, LANES), 1) < CAP

    def pair(row, n):
        return jnp.where(left, info_recv[2 * n, row : row + 1, :], info_recv[2 * n + 1, row : row + 1, :])

    for n in range(16):
        spots[32 + n : 33 + n, :] = place(pair(2, n))
        cols = jnp.broadcast_to(pair(1, n).astype(F32), (LANES, LANES)).T.astype(I32)
        for q in range(4):
            pick_d[n * LANES : (n + 1) * LANES, q * LANES : (q + 1) * LANES] = jnp.where(
                at_lane + q * LANES == cols, 1.0, 0.0
            ).astype(BF16)

    wait_bytes(db_recv.at[1:OWNERS], sems.at[3])
    for m in range(2):
        acc = jnp.zeros((256, D), F32)
        for p in range(4):
            rows = [pair(0, 4 * p + s) for s in range(4)]
            blocks = db_recv[8 * p : 8 * (p + 1)].reshape(512, D)
            acc = acc + dot(one_hot(rows, 256, 256 * m), blocks)
        part_db[256 * m : 256 * (m + 1), :] = acc

    across(part_db, got_db, 10)
    wait_bytes(got_db, sems.at[11])
    quarter_db[...] = part_db[quarter(x), :] + got_db[0] + got_db[1] + got_db[2]
    all_quarters(quarter_db, full_db, 12)
    full_db[quarter(x), :] = quarter_db[...]
    wait_bytes(full_b.at[0:384], sems.at[9])
    wait_bytes(full_db.at[0:384], sems.at[13])

    for ref, value in ((table_hl, full_db[...]), (table_w, full_db[...] + full_b[...])):
        top = value.astype(BF16)
        ref[:, :D] = top
        ref[:, D:] = (value - top.astype(F32)).astype(BF16)

    def a_block(j, carry):
        at = pl.ds(pl.multiple_of(j * 256, 256), 256)
        both = dot(pick[at, :], table_hl[...])
        value = (both[:, :D] + both[:, D:]) * a_rows[at, :].astype(F32)
        terms[at, :] = value.astype(BF16)
        return carry

    lax.fori_loop(0, 16, a_block, 0)
    wait_bytes(da_recv.at[1:OWNERS], sems.at[5])

    def d_block(j, carry):
        at = pl.ds(pl.multiple_of(j * 256, 256), 256)
        both = dot(pick_d[at, :], table_w[...])
        rows = da_recv[pl.ds(4 * j, 4)].reshape(256, D)
        value = (both[:, :D] + both[:, D:]) * rows.astype(F32)
        terms[pl.ds(pl.multiple_of(ROWS + j * 256, 256), 256), :] = value.astype(BF16)
        return carry

    lax.fori_loop(0, 8, d_block, 0)

    def summed(base):
        acc = jnp.zeros((256, D), F32)
        for p in range(12):
            rows = [spots[4 * p + s : 4 * p + s + 1, :] for s in range(4)]
            acc = acc + dot(one_hot(rows, 256, base), terms[512 * p : 512 * (p + 1), :])
        return acc

    def to_partner(c):
        near_send[c] = summed(HALF + c * 256)
        send(
            near_send.at[c], near_recv.at[c], near_sems.at[0, c], near_sems.at[1, c],
            {"keys": partner, "view": x},
        ).start()

    to_partner(0)

    def group_chunk(c, carry):
        @pl.when(c < 7)
        def _():
            to_partner(c + 1)

        acc = summed(c * 256)
        wait_bytes(near_recv.at[c], near_sems.at[1, c])
        acc = acc + near_recv[c]

        @pl.when(c == 0)
        def _():
            own[...] = acc[:GROUPS_DEV, :]

        far_send[pl.ds(8 * c, 8)] = acc.astype(BF16).reshape(8, GROUPS_DEV, D)

        def block(j, carry):
            send(
                far_send.at[j], far_recv.at[PEERS - j], sems.at[14], sems.at[15], peer(j)
            ).start()
            return carry

        lax.fori_loop(lax.max(8 * c, 1), 8 * c + 8, block, 0)
        return carry

    lax.fori_loop(0, 8, group_chunk, 0)

    wait_bytes(far_recv.at[1:PEERS], sems.at[15])
    total = own[...]
    for j in range(1, PEERS):
        total = total + far_recv[j].astype(F32)
    out[...] = total

    wait_bytes(info_send.at[1:OWNERS], sems.at[0])
    wait_bytes(db_send.at[1:OWNERS], sems.at[2])
    wait_bytes(da_send.at[1:OWNERS], sems.at[4])
    wait_bytes(part_b.at[0:384], sems.at[6])
    wait_bytes(part_b.at[0:384], sems.at[8])
    wait_bytes(part_db.at[0:384], sems.at[10])
    wait_bytes(part_db.at[0:384], sems.at[12])
    wait_bytes(far_send.at[1:PEERS], sems.at[14])
    for c in range(8):
        wait_bytes(near_send.at[c], near_sems.at[0, c])


def shards(
    key_slot, a_slot, a_group, a_weight, a_payload, b_slot, b_weight, b_payload, da_key, da_group,
    da_mult, da_payload, da_count, db_key, db_mult, db_payload, db_count,
):
    vmem = pl.BlockSpec(memory_space=pltpu.VMEM)
    smem = pl.BlockSpec(memory_space=pltpu.SMEM)

    def lanes(v):
        return v.reshape(-1, LANES)

    db_send, da_send, info = pl.pallas_call(
        pack_kernel_wrapped,
        out_shape=(
            jax.ShapeDtypeStruct((OWNERS * CAP, D), BF16),
            jax.ShapeDtypeStruct((OWNERS * CAP, D), BF16),
            jax.ShapeDtypeStruct((OWNERS, 8, LANES), I32),
        ),
        in_specs=[vmem] * 6 + [smem] * 2 + [vmem] * 2,
        out_specs=(vmem,) * 3,
        scratch_shapes=[
            pltpu.VMEM((16, LANES), I32),
            pltpu.VMEM((16, LANES), F32),
            pltpu.VMEM((2, 8, DELTA), BF16),
        ],
    )(
        lanes(key_slot), lanes(da_key), lanes(da_group), lanes(da_mult), lanes(db_key),
        lanes(db_mult), da_count, db_count, da_payload, db_payload,
    )
    table = (KEYS_DEV, D)
    return pl.pallas_call(
        main_kernel,
        out_shape=jax.ShapeDtypeStruct((GROUPS_DEV, D), F32),
        in_specs=[vmem] * 10,
        out_specs=vmem,
        scratch_shapes=[
            pltpu.VMEM((OWNERS, CAP, D), BF16),
            pltpu.VMEM((OWNERS, CAP, D), BF16),
            pltpu.VMEM((OWNERS, 8, LANES), I32),
            pltpu.VMEM(table, F32),
            pltpu.VMEM(table, F32),
            pltpu.VMEM((128, D), F32),
            pltpu.VMEM((128, D), F32),
            pltpu.VMEM((3, 128, D), F32),
            pltpu.VMEM((3, 128, D), F32),
            pltpu.VMEM(table, F32),
            pltpu.VMEM(table, F32),
            pltpu.VMEM((ROWS, KEYS_DEV), BF16),
            pltpu.VMEM((OWNERS * CAP, KEYS_DEV), BF16),
            pltpu.VMEM((KEYS_DEV, 2 * D), BF16),
            pltpu.VMEM((KEYS_DEV, 2 * D), BF16),
            pltpu.VMEM((ROWS + OWNERS * CAP, D), BF16),
            pltpu.VMEM((48, LANES), I32),
            pltpu.VMEM((8, 256, D), F32),
            pltpu.VMEM((8, 256, D), F32),
            pltpu.VMEM((PEERS, GROUPS_DEV, D), BF16),
            pltpu.VMEM((PEERS, GROUPS_DEV, D), BF16),
            pltpu.VMEM((GROUPS_DEV, D), F32),
            pltpu.SemaphoreType.DMA((16,)),
            pltpu.SemaphoreType.DMA((2, 8)),
        ],
        compiler_params=pltpu.CompilerParams(
            collective_id=0, has_side_effects=True, vmem_limit_bytes=56 * 1024 * 1024
        ),
    )(
        db_send.reshape(OWNERS, CAP, D), da_send.reshape(OWNERS, CAP, D), info, b_payload,
        lanes(b_slot), lanes(b_weight), a_payload, lanes(a_slot), lanes(a_weight), lanes(a_group),
    )


def pack_kernel_wrapped(
    key_slot, da_key, da_group, da_mult, db_key, db_mult, da_count, db_count, da_rows, db_rows,
    db_out, da_out, info_out, spot_ref, sign_ref, info_ref,
):
    pack_kernel(
        key_slot, da_key, da_group, da_mult, db_key, db_mult, da_count, db_count, da_rows, db_rows,
        da_out, db_out, info_out, spot_ref, sign_ref, info_ref,
    )


def solution(mesh):
    rows = P(("keys", "view"))
    wide = P(("keys", "view"), None)
    placed = (
        P(), rows, rows, rows, wide, rows, rows, wide, rows, rows, rows, wide, rows, rows, rows,
        wide, rows,
    )
    return jax.shard_map(
        shards, mesh=mesh, in_specs=placed, out_specs=wide, check_vma=False
    )
```

time: 394 us -> 102 us (0.26)
  waiting for transfers between devices: 132 us -> 0 us
  other arithmetic: 119 us -> 0 us
  Pallas kernels: 0 us -> 99 us
  local copies, waits for them, and re-layouts: 87.7 us -> 1.38 us
  starting transfers between devices: 37.6 us -> 0 us
  between operations: 15.1 us -> 1.31 us
    pallas_call x0 -> x2, Pallas kernels: none -> 99 us  [the longest x1 89.8 us: shards(): pl.pallas_call(main_kernel, out_shape=jax.ShapeDtypeStruct((GROUPS_DEV, D...]
    reduce_scatter x4 -> x0, waiting for transfers between devices: 91.5 us -> none  [own_block(): blocks = lax.psum_scatter(blocks, axes[k], scatter_dimension=0, tiled=True)]
    scatter-add x3 -> x0, other arithmetic: 79.1 us -> none  [the longest x1 40.1 us: shards(): jax.ops.segment_sum(all_terms.astype(jnp.float32), segment_index, num_seg...]
    gather x6 -> x0, local copies, waits for them, and re-layouts: 52.3 us -> none  [the longest x2 17.3 us: pack_rows(): slot_rank = jnp.take_along_axis(before, target[:, None], axis=1)[:, 0]]
    all_to_all x5 -> x0, waiting for transfers between devices: 40.8 us -> none  [the longest x1 40.8 us: sent_to_all(): lax.all_to_all(jnp.broadcast_to(shard[None], (size, *shard.shape)), axis,...]
    all_to_all x5 -> x0, starting transfers between devices: 37.2 us -> none  [the longest x1 9.59 us: shards(): lax.all_to_all(b_columns, KEYS, split_axis=0, concat_axis=0, tiled=True)]
    another operation x8 -> x0, other arithmetic: 18.3 us -> none
    scatter x4 -> x0, local copies, waits for them, and re-layouts: 17.9 us -> none  [the longest x2 11.3 us: pack_rows(): sent_payload = jnp.zeros((owners * capacity + 1, payload.shape[1]), paylo...]
  transfers between devices with their start and end apart: 9 -> 0, of which waited for: 5 -> 0; matrix products, arithmetic and copies ran while one was open for 30% -> 0% of each run, Pallas kernels for 0% -> 0%
where the time goes in v1:
time: 102 us
  Pallas kernels  99 us (97%)
  local copies, waits for them, and re-layouts  1.38 us (1%)
  between operations  1.31 us (1%)
    pallas_call x1, Pallas kernels, shards(): pl.pallas_call(main_kernel, out_shape=jax.ShapeDtypeStruct((GROUPS_DEV, D...  89.8 us
    pallas_call x1, Pallas kernels, shards(): pl.pallas_call(pack_kernel_wrapped, out_shape=(jax.ShapeDtypeStruct((OWNE...  9.16 us

profile of v1, /device:TPU:1, one launch (start us, length us, event | category | flops | bytes accessed | tf_op | source)
XLA Modules:
  0.0 101.7 jit_solution(8256644801903137046)
XLA Ops:
  1.3 9.2 %shard_map.163 = (bf16[2048,256]{1,0:T(8,128)(2,1)}, bf16[2048,256]{1,0:T(8,128)(2,1)}, s32[32,8,128]{2,1,0:T(8,128)}) custom-call(s32[128,128]{1,0:T(8,128)} %bitcast.15, s32[8,128]{1,0:T(8,128)} %bitcast.21, s32[8,128]{1,0:T(8,128)} %bitcast.22, s32[8,128]{1,0:T(8,128)} %bitcast.23, s32[8,128]{1,0:T(8,128)} %bitcast.24, s32[8,128]{1,0:T(8,128)} %bitcast.25, ...), custom_call_target="tpu_custom_call" | custom-call | tf_op jit(solution)/shard_map/pallas_call | solution.py:381
  10.5 89.8 %shard_map.164 = f32[32,256]{1,0:T(8,128)} custom-call(bf16[32,64,256]{2,1,0:T(8,128)(2,1)} %bitcast.13, bf16[32,64,256]{2,1,0:T(8,128)(2,1)} %bitcast.14, s32[32,8,128]{2,1,0:T(8,128)} %get-tuple-element.10.info_send, bf16[4096,256]{1,0:T(8,128)(2,1)} %b_rows.1, s32[32,128]{1,0:T(8,128)} %bitcast.16, s32[32,128]{1,0:T(8,128)} %bitcast.17, ...), custom_call_target="tpu_custom_call" | custom-call | tf_op jit(solution)/shard_map/pallas_call | solution.py:400
  100.3 1.4 %copy.21 = f32[32,256]{1,0:T(8,128)} copy(f32[32,256]{1,0:T(8,128)} %shard_map.164) | data formatting | bytes 65536

commit v2 on v1

v2 whole, which is shorter than its diff:
```python
import jax
import jax.numpy as jnp
from jax import lax
from jax.experimental import pallas as pl
from jax.experimental.pallas import tpu as pltpu
from jax.sharding import PartitionSpec as P

MESH = pl.DeviceIdType.MESH
F32, BF16, I32 = jnp.float32, jnp.bfloat16, jnp.int32
D = 256
KEYS_DEV = 512
GROUPS_DEV = 32
ROWS = 4096
DELTA = 1024
CAP = 64
OWNERS = 32
VIEWS = 4
LANES = 128
PEERS = 64
HALF = 2048
OWNER_STEP = 11
PEER_STEP, PEER_STEP_INVERSE = 27, 19


def iota(shape, dim):
    return lax.broadcasted_iota(I32, shape, dim)


def dot(a, b):
    return jnp.dot(a, b, preferred_element_type=F32)


def one_hot(rows, height, base, values=None):
    at = iota((height, LANES), 0)
    parts = []
    for n, row in enumerate(rows):
        value = 1.0 if values is None else values[n]
        parts.append(jnp.where(at == row - base, value, 0.0).astype(BF16))
    return jnp.concatenate(parts, axis=1)


def places(table, key_ref, count):
    keys = [key_ref[s : s + 1, :] for s in range(DELTA // LANES)]
    at = iota((LANES, LANES), 0)
    hits = jnp.concatenate(
        [jnp.where(at == (k >> 7), 1.0, 0.0).astype(BF16) for k in keys], axis=1
    )
    found = dot(table, hits)
    slots, owners, lives, marks = [], [], [], []
    lane = iota((1, LANES), 1)
    owner_at = iota((OWNERS, LANES), 0)
    for s, k in enumerate(keys):
        cut = slice(s * LANES, (s + 1) * LANES)
        value = found[:LANES, cut] * 128.0 + found[LANES:, cut]
        slot = jnp.sum(jnp.where(at == (k & 127), value, 0.0), axis=0, keepdims=True).astype(I32)
        live = lane + s * LANES < count
        owner = jnp.where(live, slot >> 9, -1)
        slots.append(slot & (KEYS_DEV - 1))
        owners.append(owner)
        lives.append(live)
        marks.append(jnp.where(owner_at == owner, 1.0, 0.0))
    stacked = jnp.concatenate(marks, axis=0).astype(BF16)
    col = iota((LANES, 2 * LANES), 1)
    before = jnp.where((iota((LANES, 2 * LANES), 0) < col) | (col >= LANES), 1.0, 0.0).astype(BF16)
    counts = dot(stacked, before)
    carry = jnp.zeros((OWNERS, LANES), F32)
    spots = []
    for s in range(len(keys)):
        cut = slice(s * OWNERS, (s + 1) * OWNERS)
        rank = jnp.sum(marks[s] * (counts[cut, :LANES] + carry), axis=0, keepdims=True).astype(I32)
        spots.append(jnp.where(lives[s], owners[s] * CAP + rank, -1))
        carry = carry + counts[cut, LANES:]
    return slots, spots


def wait_bytes(ref, sem):
    pltpu.make_async_copy(ref, ref, sem).wait()


def kernel(
    key_slot, da_key, da_group, da_mult, da_count, db_key, db_mult, db_count, b_slot, b_weight,
    a_slot, a_weight, a_group, da_hbm, db_hbm, b_hbm, a_hbm,
    out,
    da_rows, db_rows, b_rows, a_rows, spot_ref, sign_ref, note_ref,
    db_send, da_send, db_info, da_info, db_recv, da_recv, db_info_recv, da_info_recv,
    part_b, quarter_b, got_b, full_b, part_db, quarter_db, got_db, full_db,
    pick, pick_d, table_a, table_w, terms, spots, near_send, near_recv, far_send, far_recv, own,
    load_sems, sems, near_sems,
):
    k, x = lax.axis_index("keys"), lax.axis_index("view")
    core = lax.rem(k, 2)
    partner = k + 1 - 2 * core
    seat = (k // 2) * VIEWS + x

    def load(src, dst, s):
        return pltpu.make_async_copy(src, dst, load_sems.at[s])

    loads = [
        load(db_hbm, db_rows, 0),
        load(da_hbm, da_rows, 1),
        load(b_hbm, b_rows, 2),
        load(a_hbm, a_rows, 3),
    ]
    for copy in loads:
        copy.start()

    def peer(j):
        t = lax.rem(seat + j, PEERS)
        return {"keys": (t // VIEWS) * 2 + core, "view": lax.rem(t, VIEWS)}

    def send(src, dst, sem_s, sem_r, device):
        return pltpu.make_async_remote_copy(
            src_ref=src, dst_ref=dst, send_sem=sem_s, recv_sem=sem_r, device_id=device,
            device_id_type=MESH,
        )

    barrier = pltpu.get_barrier_semaphore()

    def greet_same(j, carry):
        pl.semaphore_signal(barrier, inc=1, device_id=peer(j), device_id_type=MESH)
        return carry

    def greet_other(j, carry):
        to = {"keys": lax.rem(k + 2 * j + 1, OWNERS), "view": x}
        pl.semaphore_signal(barrier, inc=1, device_id=to, device_id_type=MESH)
        return carry

    with jax.named_scope("greet"):
        lax.fori_loop(1, PEERS, greet_same, 0)
        lax.fori_loop(0, OWNERS // 2, greet_other, 0)

    with jax.named_scope("lookup_b"):
        whole = key_slot[...]
        high = (whole >> 7).astype(F32).T
        low = (whole & 127).astype(F32).T
        table = jnp.concatenate([high, low], axis=0).astype(BF16)

        def look_up(r, key_ref, mult_ref, count_ref):
            slots, found = places(table, key_ref, count_ref[...])
            for s in range(8):
                cut = slice(s * LANES, (s + 1) * LANES)
                spot_ref[8 * r + s : 8 * r + s + 1, :] = found[s]
                sign_ref[8 * r + s : 8 * r + s + 1, :] = mult_ref[s : s + 1, :].astype(F32)
                group = da_group[s : s + 1, :]
                rows = [slots[s] >> 4, slots[s] & 15, group >> 6, group & 63]
                zero = jnp.zeros((4, LANES), F32)
                note_ref[r, :, cut] = jnp.concatenate(
                    [row.astype(F32) for row in rows] + [zero], axis=0
                ).astype(BF16)

        look_up(0, db_key, db_mult, db_count)

    def owner_of(i):
        return lax.rem(k + lax.rem(OWNER_STEP * i, OWNERS), OWNERS)

    def home(i):
        return lax.rem(OWNERS - lax.rem(OWNER_STEP * i, OWNERS), OWNERS)

    first = iota((8, LANES), 1) < CAP

    def packed(r, i, rows):
        at = iota((CAP, LANES), 0)
        picks = []
        for q in range(4):
            base = owner_of(4 * i + q) * CAP
            parts = []
            for s in range(8):
                spot = spot_ref[8 * r + s : 8 * r + s + 1, :]
                sign = sign_ref[8 * r + s : 8 * r + s + 1, :]
                parts.append(jnp.where(at == spot - base, sign, 0.0).astype(BF16))
            picks.append(jnp.concatenate(parts, axis=1))
        pick_rows = jnp.concatenate(picks, axis=0)
        blocks = dot(pick_rows, rows[...]).astype(BF16)
        note = jnp.abs(
            lax.dot_general(
                note_ref[r], pick_rows, (((1,), (1,)), ((), ())), preferred_element_type=F32
            )
        )
        info = jnp.concatenate(
            [
                note[0:1] * 16.0 + note[1:2],
                note[2:3] * 64.0 + note[3:4],
                jnp.zeros((6, 256), F32),
            ],
            axis=0,
        ).astype(I32)
        infos = []
        for q in range(4):
            v = info[:, (q // 2) * LANES : (q // 2 + 1) * LANES]
            turned = pltpu.roll(v, CAP, 1)
            infos.append(jnp.where(first, v, turned) if q % 2 == 0 else jnp.where(first, turned, v))
        return blocks, infos

    loads[0].wait()
    with jax.named_scope("barrier"):
        pl.semaphore_wait(barrier, PEERS - 1 + OWNERS // 2)

    def pack_b(i, carry):
        blocks, infos = packed(0, i, db_rows)
        for q in range(4):
            n = 4 * i + q
            db_info[n] = infos[q][0:1]
            for h in range(2):
                db_send[h, n] = blocks[q * CAP : (q + 1) * CAP, h * LANES : (h + 1) * LANES]
        for q in range(4):
            n = 4 * i + q

            @pl.when(n > 0)
            def _():
                to = {"keys": owner_of(n), "view": x}
                send(db_info.at[n], db_info_recv.at[home(n)], sems.at[0], sems.at[1], to).start()
                send(db_send.at[0, n], db_recv.at[0, home(n)], sems.at[2], sems.at[3], to).start()

        return carry

    with jax.named_scope("pack_b"):
        lax.fori_loop(0, 8, pack_b, 0)

    def second_half(n, carry):
        to = {"keys": owner_of(n), "view": x}
        send(db_send.at[1, n], db_recv.at[1, home(n)], sems.at[4], sems.at[5], to).start()
        return carry

    lax.fori_loop(1, OWNERS, second_half, 0)
    db_info_recv[0] = db_info[0]
    db_recv[0, 0] = db_send[0, 0]
    db_recv[1, 0] = db_send[1, 0]

    def quarter(at):
        return pl.ds(pl.multiple_of(at * 128, 128), 128)

    def across(part, got, s):
        for j in range(1, VIEWS):
            to = lax.rem(x + j, VIEWS)
            send(
                part.at[quarter(to)], got.at[j - 1], sems.at[s], sems.at[s + 1],
                {"keys": k, "view": to},
            ).start()

    def all_quarters(mine, full, s):
        for j in range(1, VIEWS):
            to = lax.rem(x + j, VIEWS)
            send(
                mine, full.at[quarter(x)], sems.at[s], sems.at[s + 1], {"keys": k, "view": to}
            ).start()

    loads[2].wait()
    with jax.named_scope("sum_b"):
        for m in range(2):
            acc = jnp.zeros((256, D), F32)
            for p in range(8):
                rows = [b_slot[4 * p + s : 4 * p + s + 1, :] for s in range(4)]
                values = [b_weight[4 * p + s : 4 * p + s + 1, :].astype(F32) for s in range(4)]
                hits = one_hot(rows, 256, 256 * m, values)
                acc = acc + dot(hits, b_rows[512 * p : 512 * (p + 1), :])
            part_b[256 * m : 256 * (m + 1), :] = acc
        across(part_b, got_b, 8)

    with jax.named_scope("lookup_a"):
        look_up(1, da_key, da_mult, da_count)
    loads[1].wait()

    def pack_a(i, carry):
        blocks, infos = packed(1, i, da_rows)
        for q in range(4):
            da_info[4 * i + q] = infos[q][0:2]
            da_send[4 * i + q] = blocks[q * CAP : (q + 1) * CAP, :]
        return carry

    with jax.named_scope("pack_a"):
        lax.fori_loop(0, 8, pack_a, 0)

    with jax.named_scope("wait_b"):
        wait_bytes(got_b, sems.at[9])
    quarter_b[...] = part_b[quarter(x), :] + got_b[0] + got_b[1] + got_b[2]
    all_quarters(quarter_b, full_b, 10)
    full_b[quarter(x), :] = quarter_b[...]

    left = iota((1, LANES), 1) < CAP

    def pair(ref, row, n):
        return jnp.where(left, ref[2 * n, row : row + 1, :], ref[2 * n + 1, row : row + 1, :])

    def sum_db(h):
        for m in range(2):
            acc = jnp.zeros((256, LANES), F32)
            for p in range(4):
                rows = [pair(db_info_recv, 0, 4 * p + s) for s in range(4)]
                blocks = db_recv[h, 8 * p : 8 * (p + 1)].reshape(512, LANES)
                acc = acc + dot(one_hot(rows, 256, 256 * m), blocks)
            part_db[h, 256 * m : 256 * (m + 1), :] = acc

    def finish_quarter(h):
        quarter_db[h] = part_db[h, quarter(x), :] + got_db[h, 0] + got_db[h, 1] + got_db[h, 2]
        all_quarters(quarter_db.at[h], full_db.at[h], 16 + 4 * h)
        full_db[h, quarter(x), :] = quarter_db[h]

    with jax.named_scope("wait_db0"):
        wait_bytes(db_info_recv.at[1:OWNERS], sems.at[1])
        wait_bytes(db_recv.at[0, 1:OWNERS], sems.at[3])
    sum_db(0)
    across(part_db.at[0], got_db.at[0], 14)

    at_lane = iota((LANES, LANES), 1)

    def pick_block(j, carry):
        row = a_slot[pl.ds(j, 1), :] + KEYS_DEV * a_weight[pl.ds(j, 1), :]
        cols = jnp.broadcast_to(row.astype(F32), (LANES, LANES)).T.astype(I32)
        slot, weight = cols & (KEYS_DEV - 1), (cols >> 9).astype(F32)
        at = pl.ds(pl.multiple_of(j * LANES, LANES), LANES)
        for q in range(4):
            pick[at, q * LANES : (q + 1) * LANES] = jnp.where(
                at_lane + q * LANES == slot, weight, 0.0
            ).astype(BF16)
        return carry

    with jax.named_scope("pick"):
        lax.fori_loop(0, 32, pick_block, 0)

    def place(group):
        device = group >> 5
        seat_g = (device >> 3) * VIEWS + (device & 3)
        other = ((device >> 2) & 1) ^ core
        turn = ((seat_g - seat) * PEER_STEP_INVERSE) & (PEERS - 1)
        return other * HALF + turn * GROUPS_DEV + (group & 31)

    spots[0:32, :] = place(a_group[...])

    with jax.named_scope("wait_rs0"):
        wait_bytes(got_db.at[0], sems.at[15])
    finish_quarter(0)

    with jax.named_scope("wait_db1"):
        wait_bytes(db_recv.at[1, 1:OWNERS], sems.at[5])
    sum_db(1)
    across(part_db.at[1], got_db.at[1], 18)

    def send_a(n, carry):
        to = {"keys": owner_of(n), "view": x}
        send(da_info.at[n], da_info_recv.at[home(n)], sems.at[6], sems.at[7], to).start()
        send(da_send.at[n], da_recv.at[home(n)], sems.at[12], sems.at[13], to).start()
        return carry

    lax.fori_loop(1, OWNERS, send_a, 0)
    da_info_recv[0] = da_info[0]
    da_recv[0] = da_send[0]

    def split(value):
        top = value.astype(BF16)
        return jnp.concatenate([top, (value - top.astype(F32)).astype(BF16)], axis=1)

    def a_terms(h):
        table_a[h] = split(full_db[h])

        def block(j, carry):
            at = pl.ds(pl.multiple_of(j * 1024, 1024), 1024)
            cut = slice(h * LANES, (h + 1) * LANES)
            both = dot(pick[at, :], table_a[h])
            value = (both[:, :LANES] + both[:, LANES:]) * a_rows[at, cut].astype(F32)
            terms[at, cut] = value.astype(BF16)
            return carry

        lax.fori_loop(0, 4, block, 0)

    loads[3].wait()
    with jax.named_scope("wait_ag0"):
        wait_bytes(full_db.at[0, 0:384], sems.at[17])
    with jax.named_scope("a_terms0"):
        a_terms(0)
    with jax.named_scope("wait_rs1"):
        wait_bytes(got_db.at[1], sems.at[19])
    finish_quarter(1)

    with jax.named_scope("wait_ag1"):
        wait_bytes(full_b.at[0:384], sems.at[11])
        wait_bytes(full_db.at[1, 0:384], sems.at[21])
    with jax.named_scope("a_terms1"):
        a_terms(1)

    for h in range(2):
        table_w[h] = split(full_db[h] + full_b[:, h * LANES : (h + 1) * LANES])

    with jax.named_scope("wait_da"):
        wait_bytes(da_info_recv.at[1:OWNERS], sems.at[7])
    with jax.named_scope("pick_d"):
        for n in range(16):
            spots[32 + n : 33 + n, :] = place(pair(da_info_recv, 1, n))
            cols = jnp.broadcast_to(
                pair(da_info_recv, 0, n).astype(F32), (LANES, LANES)
            ).T.astype(I32)
            for q in range(4):
                pick_d[n * LANES : (n + 1) * LANES, q * LANES : (q + 1) * LANES] = jnp.where(
                    at_lane + q * LANES == cols, 1.0, 0.0
                ).astype(BF16)
    with jax.named_scope("wait_da2"):
        wait_bytes(da_recv.at[1:OWNERS], sems.at[13])

    def d_block(j, carry):
        at = pl.ds(pl.multiple_of(j * 512, 512), 512)
        rows = da_recv[pl.ds(8 * j, 8)].reshape(512, D).astype(F32)
        for h in range(2):
            both = dot(pick_d[at, :], table_w[h])
            value = (both[:, :LANES] + both[:, LANES:]) * rows[:, h * LANES : (h + 1) * LANES]
            terms[
                pl.ds(pl.multiple_of(ROWS + j * 512, 512), 512), h * LANES : (h + 1) * LANES
            ] = value.astype(BF16)
        return carry

    with jax.named_scope("d_terms"):
        lax.fori_loop(0, 4, d_block, 0)

    def summed(base):
        acc = jnp.zeros((256, D), F32)
        for p in range(12):
            rows = [spots[4 * p + s : 4 * p + s + 1, :] for s in range(4)]
            acc = acc + dot(one_hot(rows, 256, base), terms[512 * p : 512 * (p + 1), :])
        return acc

    def to_partner(c):
        near_send[c] = summed(HALF + c * 256)
        send(
            near_send.at[c], near_recv.at[c], near_sems.at[0, c], near_sems.at[1, c],
            {"keys": partner, "view": x},
        ).start()

    def group_chunk(c, carry):
        @pl.when(c < 7)
        def _():
            to_partner(c + 1)

        acc = summed(c * 256)
        wait_bytes(near_recv.at[c], near_sems.at[1, c])
        acc = acc + near_recv[c]

        @pl.when(c == 0)
        def _():
            own[...] = acc[:GROUPS_DEV, :]

        far_send[pl.ds(8 * c, 8)] = acc.astype(BF16).reshape(8, GROUPS_DEV, D)

        def block(n, carry):
            j = lax.rem(PEER_STEP * n, PEERS)
            send(
                far_send.at[n], far_recv.at[PEERS - j], sems.at[22], sems.at[23], peer(j)
            ).start()
            return carry

        lax.fori_loop(lax.max(8 * c, 1), 8 * c + 8, block, 0)
        return carry

    with jax.named_scope("groups"):
        to_partner(0)
        lax.fori_loop(0, 8, group_chunk, 0)

    with jax.named_scope("wait_far"):
        wait_bytes(far_recv.at[1:PEERS], sems.at[23])
    with jax.named_scope("tail"):
        total = own[...]
        for j in range(1, PEERS):
            total = total + far_recv[j].astype(F32)
        out[...] = total

    wait_bytes(db_info.at[1:OWNERS], sems.at[0])
    wait_bytes(db_send.at[0, 1:OWNERS], sems.at[2])
    wait_bytes(db_send.at[1, 1:OWNERS], sems.at[4])
    wait_bytes(da_info.at[1:OWNERS], sems.at[6])
    wait_bytes(part_b.at[0:384], sems.at[8])
    wait_bytes(part_b.at[0:384], sems.at[10])
    wait_bytes(da_send.at[1:OWNERS], sems.at[12])
    for h in range(2):
        wait_bytes(part_db.at[h, 0:384], sems.at[14 + 4 * h])
        wait_bytes(part_db.at[h, 0:384], sems.at[16 + 4 * h])
    wait_bytes(far_send.at[1:PEERS], sems.at[22])
    for c in range(8):
        wait_bytes(near_send.at[c], near_sems.at[0, c])


def shards(
    key_slot, a_slot, a_group, a_weight, a_payload, b_slot, b_weight, b_payload, da_key, da_group,
    da_mult, da_payload, da_count, db_key, db_mult, db_payload, db_count,
):
    vmem = pl.BlockSpec(memory_space=pltpu.VMEM)
    hbm = pl.BlockSpec(memory_space=pl.ANY)

    def lanes(v):
        return v.reshape(-1, LANES)

    def one(v):
        return v.reshape(1, 1)

    def held(*shape, dtype=F32):
        return pltpu.VMEM(shape, dtype)

    return pl.pallas_call(
        kernel,
        out_shape=jax.ShapeDtypeStruct((GROUPS_DEV, D), F32),
        in_specs=[vmem] * 13 + [hbm] * 4,
        out_specs=vmem,
        scratch_shapes=[
            held(DELTA, D, dtype=BF16),
            held(DELTA, D, dtype=BF16),
            held(ROWS, D, dtype=BF16),
            held(ROWS, D, dtype=BF16),
            held(16, LANES, dtype=I32),
            held(16, LANES),
            held(2, 8, DELTA, dtype=BF16),
            held(2, OWNERS, CAP, LANES, dtype=BF16),
            held(OWNERS, CAP, D, dtype=BF16),
            held(OWNERS, 1, LANES, dtype=I32),
            held(OWNERS, 2, LANES, dtype=I32),
            held(2, OWNERS, CAP, LANES, dtype=BF16),
            held(OWNERS, CAP, D, dtype=BF16),
            held(OWNERS, 1, LANES, dtype=I32),
            held(OWNERS, 2, LANES, dtype=I32),
            held(KEYS_DEV, D),
            held(128, D),
            held(3, 128, D),
            held(KEYS_DEV, D),
            held(2, KEYS_DEV, LANES),
            held(2, 128, LANES),
            held(2, 3, 128, LANES),
            held(2, KEYS_DEV, LANES),
            held(ROWS, KEYS_DEV, dtype=BF16),
            held(OWNERS * CAP, KEYS_DEV, dtype=BF16),
            held(2, KEYS_DEV, D, dtype=BF16),
            held(2, KEYS_DEV, D, dtype=BF16),
            held(ROWS + OWNERS * CAP, D, dtype=BF16),
            held(48, LANES, dtype=I32),
            held(8, 256, D),
            held(8, 256, D),
            held(PEERS, GROUPS_DEV, D, dtype=BF16),
            held(PEERS, GROUPS_DEV, D, dtype=BF16),
            held(GROUPS_DEV, D),
            pltpu.SemaphoreType.DMA((4,)),
            pltpu.SemaphoreType.DMA((24,)),
            pltpu.SemaphoreType.DMA((2, 8)),
        ],
        compiler_params=pltpu.CompilerParams(
            collective_id=0, has_side_effects=True, vmem_limit_bytes=56 * 1024 * 1024
        ),
    )(
        lanes(key_slot), lanes(da_key), lanes(da_group), lanes(da_mult), one(da_count),
        lanes(db_key), lanes(db_mult), one(db_count), lanes(b_slot), lanes(b_weight),
        lanes(a_slot), lanes(a_weight), lanes(a_group), da_payload, db_payload, b_payload,
        a_payload,
    )


def solution(mesh):
    rows = P(("keys", "view"))
    wide = P(("keys", "view"), None)
    placed = (
        P(), rows, rows, rows, wide, rows, rows, wide, rows, rows, rows, wide, rows, rows, rows,
        wide, rows,
    )
    return jax.shard_map(
        shards, mesh=mesh, in_specs=placed, out_specs=wide, check_vma=False
    )
```

time: 102 us -> 80.2 us (0.79)
  Pallas kernels: 99 us -> 77.3 us
    pallas_call x2 -> x1, Pallas kernels: 99 us -> 77.3 us  [shards(): pl.pallas_call(kernel, out_shape=jax.ShapeDtypeStruct((GROUPS_DEV, D), F3...]
where the time goes in v2:
time: 80.2 us; the launch traced here: 80 us
  Pallas kernels  77.3 us (96%)
  local copies, waits for them, and re-layouts  1.38 us (2%)
  between operations  1.3 us (2%)
    pallas_call x1, Pallas kernels, shards(): pl.pallas_call(kernel, out_shape=jax.ShapeDtypeStruct((GROUPS_DEV, D), F3...  77.3 us

profile of v2, /device:TPU:1, one launch (start us, length us, event | category | flops | bytes accessed | tf_op | source)
XLA Modules:
  0.0 80.0 jit_solution(10960524112647776184)
XLA Ops:
  1.3 77.3 %shard_map.163 = f32[32,256]{1,0:T(8,128)} custom-call(s32[128,128]{1,0:T(8,128)} %bitcast.15, s32[8,128]{1,0:T(8,128)} %bitcast.21, s32[8,128]{1,0:T(8,128)} %bitcast.22, s32[8,128]{1,0:T(8,128)} %bitcast.23, s32[1,1]{1,0:T(1,128)} %bitcast.13.da_count, s32[8,128]{1,0:T(8,128)} %bitcast.24, s32[8,128]{1,0:T(8,128)} %bitcast.25, s32[1,1]{1,0:T(1,128)} %bitcast.14.db_count, ...), custom_call_target="tpu_custom_call" | custom-call | tf_op jit(solution)/shard_map/pallas_call | solution.py:494
  78.6 1.4 %copy.21 = f32[32,256]{1,0:T(8,128)} copy(f32[32,256]{1,0:T(8,128)} %shard_map.163) | data formatting | bytes 65536

commit v3 on v2

v3 whole, which is shorter than its diff:
```python
import jax
import jax.numpy as jnp
from jax import lax
from jax.experimental import pallas as pl
from jax.experimental.pallas import tpu as pltpu
from jax.sharding import PartitionSpec as P

MESH = pl.DeviceIdType.MESH
F32, BF16, I32 = jnp.float32, jnp.bfloat16, jnp.int32
D = 256
KEYS_DEV = 512
GROUPS_DEV = 32
ROWS = 4096
DELTA = 1024
CAP = 64
OWNERS = 32
VIEWS = 4
LANES = 128
PEERS = 64
HALF = 2048
OWNER_STEP = 11
CHUNK = 512


def apart(code):
    return sum((0, 1, 2, 1)[d] for d in (code >> 4, (code >> 2) & 3, code & 3))


FAR_FIRST = sorted(range(PEERS), key=lambda code: (-apart(code), (code * 27) % PEERS))
RANK = [FAR_FIRST.index(code) for code in range(PEERS)]


def iota(shape, dim):
    return lax.broadcasted_iota(I32, shape, dim)


def dot(a, b):
    return jnp.dot(a, b, preferred_element_type=F32)


def one_hot(rows, height, base, values=None):
    at = iota((height, LANES), 0)
    parts = []
    for n, row in enumerate(rows):
        value = 1.0 if values is None else values[n]
        parts.append(jnp.where(at == row - base, value, 0.0).astype(BF16))
    return jnp.concatenate(parts, axis=1)


def places(table, key_ref, count):
    keys = [key_ref[s : s + 1, :] for s in range(DELTA // LANES)]
    at = iota((LANES, LANES), 0)
    hits = jnp.concatenate(
        [jnp.where(at == (k >> 7), 1.0, 0.0).astype(BF16) for k in keys], axis=1
    )
    found = dot(table, hits)
    slots, owners, lives, marks = [], [], [], []
    lane = iota((1, LANES), 1)
    owner_at = iota((OWNERS, LANES), 0)
    for s, k in enumerate(keys):
        cut = slice(s * LANES, (s + 1) * LANES)
        value = found[:LANES, cut] * 128.0 + found[LANES:, cut]
        slot = jnp.sum(jnp.where(at == (k & 127), value, 0.0), axis=0, keepdims=True).astype(I32)
        live = lane + s * LANES < count
        owner = jnp.where(live, slot >> 9, -1)
        slots.append(slot & (KEYS_DEV - 1))
        owners.append(owner)
        lives.append(live)
        marks.append(jnp.where(owner_at == owner, 1.0, 0.0))
    stacked = jnp.concatenate(marks, axis=0).astype(BF16)
    col = iota((LANES, 2 * LANES), 1)
    before = jnp.where((iota((LANES, 2 * LANES), 0) < col) | (col >= LANES), 1.0, 0.0).astype(BF16)
    counts = dot(stacked, before)
    carry = jnp.zeros((OWNERS, LANES), F32)
    spots, ranks = [], []
    for s in range(len(keys)):
        cut = slice(s * OWNERS, (s + 1) * OWNERS)
        rank = jnp.sum(marks[s] * (counts[cut, :LANES] + carry), axis=0, keepdims=True).astype(I32)
        ranks.append(rank)
        spots.append(jnp.where(lives[s], owners[s] * CAP + rank, -1))
        carry = carry + counts[cut, LANES:]
    return slots, spots, marks, ranks


def by_place(marks, ranks, values):
    rank_at = iota((LANES, LANES), 0) & (CAP - 1)
    there = jnp.concatenate(
        [jnp.where(rank_at == rank, 1.0, 0.0).astype(BF16) for rank in ranks], axis=1
    )
    rows = jnp.concatenate(
        [
            jnp.concatenate([mark * v.astype(F32) for mark, v in zip(marks, value)], axis=1)
            for value in values
        ],
        axis=0,
    ).astype(BF16)
    return lax.dot_general(rows, there, (((1,), (1,)), ((), ())), preferred_element_type=F32)


def wait_bytes(ref, sem):
    pltpu.make_async_copy(ref, ref, sem).wait()


def kernel(
    key_slot, da_key, da_group, da_mult, db_key, db_mult, b_slot, b_weight, a_slot, a_weight,
    a_group, da_count_hbm, db_count_hbm, da_hbm, db_hbm, b_hbm, a_hbm,
    out,
    da_count, db_count, da_rows, db_rows, b_rows, a_rows, spot_ref, sign_ref,
    db_send, da_send, db_info, da_info, db_recv, da_recv, db_info_recv, da_info_recv,
    part_b, quarter_b, got_b, full_b, part_db, quarter_db, got_db, full_db,
    pick, pick_d, table_a, table_w, terms, spots, near_send, near_recv, far_send, far_recv, own, total_ref,
    load_sems, sems, near_sems, planes,
):
    k, x = lax.axis_index("keys"), lax.axis_index("view")
    core = lax.rem(k, 2)
    partner = k + 1 - 2 * core
    y, z = k // 8, lax.rem(k // 2, 4)

    def load(src, dst, s):
        return pltpu.make_async_copy(src, dst, load_sems.at[s])

    loads = [
        load(db_hbm, db_rows, 0),
        load(da_hbm, da_rows, 1),
        load(b_hbm, b_rows, 2),
        load(a_hbm, a_rows, 3),
        load(da_count_hbm, da_count, 4),
        load(db_count_hbm, db_count, 5),
    ]
    loads[5].start()
    loads[0].start()

    def peer(code):
        to_y, to_z = lax.rem(y + (code >> 4), 4), lax.rem(z + ((code >> 2) & 3), 4)
        return {"keys": (to_y * 4 + to_z) * 2 + core, "view": lax.rem(x + (code & 3), VIEWS)}

    def send(src, dst, sem_s, sem_r, device):
        return pltpu.make_async_remote_copy(
            src_ref=src, dst_ref=dst, send_sem=sem_s, recv_sem=sem_r, device_id=device,
            device_id_type=MESH,
        )

    barrier = pltpu.get_barrier_semaphore()

    def greet(j, carry):
        to = {"keys": lax.rem(k + j, OWNERS), "view": x}
        pl.semaphore_signal(barrier, inc=1, device_id=to, device_id_type=MESH)
        return carry

    with jax.named_scope("greet"):
        lax.fori_loop(1, OWNERS, greet, 0)
        for j in range(1, VIEWS):
            to = {"keys": k, "view": lax.rem(x + j, VIEWS)}
            pl.semaphore_signal(barrier, inc=1, device_id=to, device_id_type=MESH)
        for n in (4, 1, 2, 3):
            loads[n].start()

    with jax.named_scope("lookup_b"):
        whole = key_slot[...]
        high = (whole >> 7).astype(F32).T
        low = (whole & 127).astype(F32).T
        table = jnp.concatenate([high, low], axis=0).astype(BF16)

        def look_up(r, key_ref, mult_ref, count_ref):
            slots, found, marks, ranks = places(table, key_ref, count_ref[0])
            for s in range(8):
                spot_ref[8 * r + s : 8 * r + s + 1, :] = found[s]
                sign_ref[8 * r + s : 8 * r + s + 1, :] = mult_ref[s : s + 1, :].astype(F32)
            return slots, marks, ranks

        loads[5].wait()
        slots_b, marks_b, ranks_b = look_up(0, db_key, db_mult, db_count)
        note = by_place(
            marks_b, ranks_b, [[v >> 4 for v in slots_b], [v & 15 for v in slots_b]]
        )
        note = (note[:OWNERS] * 16.0 + note[OWNERS:]).astype(I32)
        for n in range(OWNERS):
            db_info[n] = note[n : n + 1, :]

    def home(i):
        return lax.rem(OWNER_STEP * i, OWNERS)

    def owner_of(i):
        code = home(i)
        to_y, to_z = lax.rem(y + code // 8, 4), lax.rem(z + lax.rem(code // 2, 4), 4)
        return (to_y * 4 + to_z) * 2 + lax.rem(core + lax.rem(code, 2), 2)

    def packed(r, i, rows):
        at = iota((CAP, LANES), 0)
        picks = []
        for q in range(8):
            base = owner_of(8 * i + q) * CAP
            parts = []
            for s in range(8):
                spot = spot_ref[8 * r + s : 8 * r + s + 1, :]
                sign = sign_ref[8 * r + s : 8 * r + s + 1, :]
                parts.append(jnp.where(at == spot - base, sign, 0.0).astype(BF16))
            picks.append(jnp.concatenate(parts, axis=1))
        return dot(jnp.concatenate(picks, axis=0), rows[...]).astype(BF16)

    loads[0].wait()

    def pack_b(i, carry):
        blocks = packed(0, i, db_rows)
        for q in range(8):
            n = 8 * i + q
            for h in range(2):
                db_send[h, n] = blocks[q * CAP : (q + 1) * CAP, h * LANES : (h + 1) * LANES]
        return carry

    with jax.named_scope("pack_b"):
        lax.fori_loop(0, 4, pack_b, 0)

    with jax.named_scope("barrier"):
        pl.semaphore_wait(barrier, OWNERS - 1 + VIEWS - 1)

    def first_half(n, carry):
        to = {"keys": owner_of(n), "view": x}
        send(db_info.at[owner_of(n)], db_info_recv.at[home(n)], sems.at[0], sems.at[1], to).start()
        send(db_send.at[0, n], db_recv.at[0, home(n)], sems.at[2], sems.at[3], to).start()
        return carry

    def second_half(n, carry):
        to = {"keys": owner_of(n), "view": x}
        send(db_send.at[1, n], db_recv.at[1, home(n)], sems.at[4], sems.at[5], to).start()
        return carry

    with jax.named_scope("send_b"):
        lax.fori_loop(1, OWNERS, first_half, 0)
        for j in range(1, VIEWS):
            to = {"keys": k, "view": lax.rem(x + j, VIEWS)}
            pl.semaphore_signal(planes, inc=1, device_id=to, device_id_type=MESH)
        lax.fori_loop(1, OWNERS, second_half, 0)
    db_info_recv[0] = db_info[k]
    db_recv[0, 0] = db_send[0, 0]
    db_recv[1, 0] = db_send[1, 0]

    def quarter(at):
        return pl.ds(pl.multiple_of(at * 128, 128), 128)

    def across(part, got, s):
        for j in range(1, VIEWS):
            to = lax.rem(x + j, VIEWS)
            send(
                part.at[quarter(to)], got.at[j - 1], sems.at[s], sems.at[s + 1],
                {"keys": k, "view": to},
            ).start()

    def all_quarters(mine, full, s):
        for j in range(1, VIEWS):
            to = lax.rem(x + j, VIEWS)
            send(
                mine, full.at[quarter(x)], sems.at[s], sems.at[s + 1], {"keys": k, "view": to}
            ).start()

    loads[2].wait()
    with jax.named_scope("sum_b"):
        for m in range(2):
            acc = jnp.zeros((256, D), F32)
            for p in range(8):
                rows = [b_slot[4 * p + s : 4 * p + s + 1, :] for s in range(4)]
                values = [b_weight[4 * p + s : 4 * p + s + 1, :].astype(F32) for s in range(4)]
                hits = one_hot(rows, 256, 256 * m, values)
                acc = acc + dot(hits, b_rows[512 * p : 512 * (p + 1), :])
            part_b[256 * m : 256 * (m + 1), :] = acc
        across(part_b, got_b, 8)

    with jax.named_scope("lookup_a"):
        loads[4].wait()
        slots_a, marks_a, ranks_a = look_up(1, da_key, da_mult, da_count)
        groups = [da_group[s : s + 1, :] for s in range(8)]
        note = by_place(
            marks_a,
            ranks_a,
            [
                [v >> 4 for v in slots_a],
                [v & 15 for v in slots_a],
                [v >> 6 for v in groups],
                [v & 63 for v in groups],
            ],
        )
        slot_note = (note[:OWNERS] * 16.0 + note[OWNERS : 2 * OWNERS]).astype(I32)
        group_note = (note[2 * OWNERS : 3 * OWNERS] * 64.0 + note[3 * OWNERS :]).astype(I32)
        for n in range(OWNERS):
            da_info[n] = jnp.concatenate([slot_note[n : n + 1, :], group_note[n : n + 1, :]], axis=0)
    loads[1].wait()

    def pack_a(i, carry):
        blocks = packed(1, i, da_rows)
        for q in range(8):
            da_send[8 * i + q] = blocks[q * CAP : (q + 1) * CAP, :]
        return carry

    with jax.named_scope("pack_a"):
        lax.fori_loop(0, 4, pack_a, 0)

    def send_a_info(n, carry):
        to = {"keys": owner_of(n), "view": x}
        send(da_info.at[owner_of(n)], da_info_recv.at[home(n)], sems.at[6], sems.at[7], to).start()
        return carry

    lax.fori_loop(1, OWNERS, send_a_info, 0)
    da_info_recv[0] = da_info[k]
    da_recv[0] = da_send[0]

    left = iota((1, LANES), 1) < CAP

    def pair(ref, row, n):
        return jnp.where(left, ref[2 * n, row : row + 1, :], ref[2 * n + 1, row : row + 1, :])

    def sum_db(h):
        for m in range(2):
            acc = jnp.zeros((256, LANES), F32)
            for p in range(4):
                rows = [pair(db_info_recv, 0, 4 * p + s) for s in range(4)]
                blocks = db_recv[h, 8 * p : 8 * (p + 1)].reshape(512, LANES)
                acc = acc + dot(one_hot(rows, 256, 256 * m), blocks)
            part_db[h, 256 * m : 256 * (m + 1), :] = acc

    def finish_quarter(h):
        quarter_db[h] = part_db[h, quarter(x), :] + got_db[h, 0] + got_db[h, 1] + got_db[h, 2]
        all_quarters(quarter_db.at[h], full_db.at[h], 16 + 4 * h)
        full_db[h, quarter(x), :] = quarter_db[h]

    with jax.named_scope("wait_db0"):
        wait_bytes(db_info_recv.at[1:OWNERS], sems.at[1])
        wait_bytes(db_recv.at[0, 1:OWNERS], sems.at[3])
    sum_db(0)
    across(part_db.at[0], got_db.at[0], 14)

    with jax.named_scope("wait_b"):
        wait_bytes(got_b, sems.at[9])
    whole_b = part_b[quarter(x), :] + got_b[0] + got_b[1] + got_b[2]
    for h in range(2):
        quarter_b[h] = whole_b[:, h * LANES : (h + 1) * LANES]
        full_b[h, quarter(x), :] = quarter_b[h]
    all_quarters(quarter_b.at[0], full_b.at[0], 10)

    at_lane = iota((LANES, LANES), 1)

    def pick_block(j, carry):
        row = a_slot[pl.ds(j, 1), :] + KEYS_DEV * a_weight[pl.ds(j, 1), :]
        cols = jnp.broadcast_to(row.astype(F32), (LANES, LANES)).T.astype(I32)
        slot, weight = cols & (KEYS_DEV - 1), (cols >> 9).astype(F32)
        at = pl.ds(pl.multiple_of(j * LANES, LANES), LANES)
        for q in range(4):
            pick[at, q * LANES : (q + 1) * LANES] = jnp.where(
                at_lane + q * LANES == slot, weight, 0.0
            ).astype(BF16)
        return carry

    with jax.named_scope("pick"):
        lax.fori_loop(0, 32, pick_block, 0)

    def place(group):
        to_y, to_z, to_x = group >> 10, (group >> 8) & 3, (group >> 5) & 3
        code = ((to_y - y) & 3) * 16 + ((to_z - z) & 3) * 4 + ((to_x - x) & 3)
        rank = jnp.zeros_like(code)
        for n in range(PEERS):
            rank = jnp.where(code == n, RANK[n], rank)
        other = ((group >> 7) & 1) ^ core
        return other * HALF + rank * GROUPS_DEV + (group & 31)

    spots[0:32, :] = place(a_group[...])

    with jax.named_scope("wait_rs0"):
        wait_bytes(got_db.at[0], sems.at[15])
    finish_quarter(0)

    with jax.named_scope("wait_db1"):
        wait_bytes(db_recv.at[1, 1:OWNERS], sems.at[5])
    sum_db(1)
    across(part_db.at[1], got_db.at[1], 18)

    def send_a(n, carry):
        to = {"keys": owner_of(n), "view": x}
        send(da_send.at[n], da_recv.at[home(n)], sems.at[12], sems.at[13], to).start()
        return carry

    lax.fori_loop(1, OWNERS, send_a, 0)

    with jax.named_scope("wait_da_info"):
        wait_bytes(da_info_recv.at[1:OWNERS], sems.at[7])
    with jax.named_scope("pick_d"):
        groups_d = jnp.concatenate([pair(da_info_recv, 1, n) for n in range(16)], axis=0)
        spots[32:48, :] = place(groups_d)
        for n in range(16):
            cols = jnp.broadcast_to(
                pair(da_info_recv, 0, n).astype(F32), (LANES, LANES)
            ).T.astype(I32)
            for q in range(4):
                pick_d[n * LANES : (n + 1) * LANES, q * LANES : (q + 1) * LANES] = jnp.where(
                    at_lane + q * LANES == cols, 1.0, 0.0
                ).astype(BF16)

    def split(value):
        top = value.astype(BF16)
        return jnp.concatenate([top, (value - top.astype(F32)).astype(BF16)], axis=1)

    def a_terms(h):
        table_a[h] = split(full_db[h])

        def block(j, carry):
            at = pl.ds(pl.multiple_of(j * 1024, 1024), 1024)
            cut = slice(h * LANES, (h + 1) * LANES)
            both = dot(pick[at, :], table_a[h])
            value = (both[:, :LANES] + both[:, LANES:]) * a_rows[at, cut].astype(F32)
            terms[at, cut] = value.astype(BF16)
            return carry

        lax.fori_loop(0, 4, block, 0)

    with jax.named_scope("wait_rs1"):
        wait_bytes(got_db.at[1], sems.at[19])
    finish_quarter(1)
    all_quarters(quarter_b.at[1], full_b.at[1], 24)

    loads[3].wait()
    with jax.named_scope("wait_ag0"):
        wait_bytes(full_db.at[0, 0:384], sems.at[17])
    with jax.named_scope("a_terms0"):
        a_terms(0)

    with jax.named_scope("wait_ag1"):
        wait_bytes(full_db.at[1, 0:384], sems.at[21])
    with jax.named_scope("a_terms1"):
        a_terms(1)

    with jax.named_scope("wait_ag_b"):
        wait_bytes(full_b.at[0, 0:384], sems.at[11])
        wait_bytes(full_b.at[1, 0:384], sems.at[25])
    for h in range(2):
        table_w[h] = split(full_db[h] + full_b[h])

    with jax.named_scope("wait_da"):
        wait_bytes(da_recv.at[1:OWNERS], sems.at[13])

    def d_block(j, carry):
        at = pl.ds(pl.multiple_of(j * 512, 512), 512)
        rows = da_recv[pl.ds(8 * j, 8)].reshape(512, D).astype(F32)
        for h in range(2):
            both = dot(pick_d[at, :], table_w[h])
            value = (both[:, :LANES] + both[:, LANES:]) * rows[:, h * LANES : (h + 1) * LANES]
            terms[
                pl.ds(pl.multiple_of(ROWS + j * 512, 512), 512), h * LANES : (h + 1) * LANES
            ] = value.astype(BF16)
        return carry

    with jax.named_scope("d_terms"):
        lax.fori_loop(0, 4, d_block, 0)

    def summed(base):
        acc = jnp.zeros((CHUNK, D), F32)
        for p in range(12):
            rows = [spots[4 * p + s : 4 * p + s + 1, :] for s in range(4)]
            acc = acc + dot(one_hot(rows, CHUNK, base), terms[512 * p : 512 * (p + 1), :])
        return acc

    chunks = HALF // CHUNK
    blocks_each = CHUNK // GROUPS_DEV
    steps = [(other, c) for c in range(chunks) for other in (1, 0)]

    def group_step(t, carry):
        base = 0
        for n, (other, c) in enumerate(steps):
            base = jnp.where(t == n, other * HALF + c * CHUNK, base)
        total_ref[...] = summed(base)
        for n, (other, c) in enumerate(steps):

            @pl.when(t == n)
            def _(other=other, c=c):
                if other:
                    near_send[c] = total_ref[...]
                    send(
                        near_send.at[c], near_recv.at[c], near_sems.at[0, c], near_sems.at[1, c],
                        {"keys": partner, "view": x},
                    ).start()
                    return
                wait_bytes(near_recv.at[c], near_sems.at[1, c])
                acc = total_ref[...] + near_recv[c]
                if c + 1 == chunks:
                    own[...] = acc[CHUNK - GROUPS_DEV :, :]
                far_send[c * blocks_each : (c + 1) * blocks_each] = acc.astype(BF16).reshape(
                    blocks_each, GROUPS_DEV, D
                )
                if c == 0:
                    pl.semaphore_wait(planes, VIEWS - 1)
                for m in range(c * blocks_each, (c + 1) * blocks_each):
                    code = FAR_FIRST[m]
                    if code:
                        send(
                            far_send.at[m], far_recv.at[code], sems.at[22], sems.at[23], peer(code)
                        ).start()

        return carry

    with jax.named_scope("groups"):
        lax.fori_loop(0, len(steps), group_step, 0)

    with jax.named_scope("wait_far"):
        wait_bytes(far_recv.at[1:PEERS], sems.at[23])
    with jax.named_scope("tail"):
        total = own[...]
        for j in range(1, PEERS):
            total = total + far_recv[j].astype(F32)
        out[...] = total

    wait_bytes(db_info.at[1:OWNERS], sems.at[0])
    wait_bytes(db_send.at[0, 1:OWNERS], sems.at[2])
    wait_bytes(db_send.at[1, 1:OWNERS], sems.at[4])
    wait_bytes(da_info.at[1:OWNERS], sems.at[6])
    wait_bytes(part_b.at[0:384], sems.at[8])
    wait_bytes(full_b.at[0, 0:384], sems.at[10])
    wait_bytes(full_b.at[1, 0:384], sems.at[24])
    wait_bytes(da_send.at[1:OWNERS], sems.at[12])
    for h in range(2):
        wait_bytes(part_db.at[h, 0:384], sems.at[14 + 4 * h])
        wait_bytes(part_db.at[h, 0:384], sems.at[16 + 4 * h])
    wait_bytes(far_send.at[0 : PEERS - 1], sems.at[22])
    for c in range(chunks):
        wait_bytes(near_send.at[c], near_sems.at[0, c])


def shards(
    key_slot, a_slot, a_group, a_weight, a_payload, b_slot, b_weight, b_payload, da_key, da_group,
    da_mult, da_payload, da_count, db_key, db_mult, db_payload, db_count,
):
    vmem = pl.BlockSpec(memory_space=pltpu.VMEM)
    hbm = pl.BlockSpec(memory_space=pl.ANY)
    fixed = pl.BlockSpec(memory_space=pltpu.HBM)

    def lanes(v):
        return v.reshape(-1, LANES)

    def held(*shape, dtype=F32):
        return pltpu.VMEM(shape, dtype)

    return pl.pallas_call(
        kernel,
        out_shape=jax.ShapeDtypeStruct((GROUPS_DEV, D), F32),
        in_specs=[vmem] * 11 + [fixed] * 2 + [hbm] * 4,
        out_specs=vmem,
        scratch_shapes=[
            pltpu.SMEM((1,), I32),
            pltpu.SMEM((1,), I32),
            held(DELTA, D, dtype=BF16),
            held(DELTA, D, dtype=BF16),
            held(ROWS, D, dtype=BF16),
            held(ROWS, D, dtype=BF16),
            held(16, LANES, dtype=I32),
            held(16, LANES),
            held(2, OWNERS, CAP, LANES, dtype=BF16),
            held(OWNERS, CAP, D, dtype=BF16),
            held(OWNERS, 1, LANES, dtype=I32),
            held(OWNERS, 2, LANES, dtype=I32),
            held(2, OWNERS, CAP, LANES, dtype=BF16),
            held(OWNERS, CAP, D, dtype=BF16),
            held(OWNERS, 1, LANES, dtype=I32),
            held(OWNERS, 2, LANES, dtype=I32),
            held(KEYS_DEV, D),
            held(2, 128, LANES),
            held(3, 128, D),
            held(2, KEYS_DEV, LANES),
            held(2, KEYS_DEV, LANES),
            held(2, 128, LANES),
            held(2, 3, 128, LANES),
            held(2, KEYS_DEV, LANES),
            held(ROWS, KEYS_DEV, dtype=BF16),
            held(OWNERS * CAP, KEYS_DEV, dtype=BF16),
            held(2, KEYS_DEV, D, dtype=BF16),
            held(2, KEYS_DEV, D, dtype=BF16),
            held(ROWS + OWNERS * CAP, D, dtype=BF16),
            held(48, LANES, dtype=I32),
            held(HALF // CHUNK, CHUNK, D),
            held(HALF // CHUNK, CHUNK, D),
            held(PEERS, GROUPS_DEV, D, dtype=BF16),
            held(PEERS, GROUPS_DEV, D, dtype=BF16),
            held(GROUPS_DEV, D),
            held(CHUNK, D),
            pltpu.SemaphoreType.DMA((6,)),
            pltpu.SemaphoreType.DMA((26,)),
            pltpu.SemaphoreType.DMA((2, HALF // CHUNK)),
            pltpu.SemaphoreType.REGULAR,
        ],
        compiler_params=pltpu.CompilerParams(
            collective_id=0, has_side_effects=True, vmem_limit_bytes=56 * 1024 * 1024
        ),
    )(
        lanes(key_slot), lanes(da_key), lanes(da_group), lanes(da_mult), lanes(db_key),
        lanes(db_mult), lanes(b_slot), lanes(b_weight), lanes(a_slot), lanes(a_weight),
        lanes(a_group), da_count, db_count, da_payload, db_payload, b_payload, a_payload,
    )


def solution(mesh):
    rows = P(("keys", "view"))
    wide = P(("keys", "view"), None)
    placed = (
        P(), rows, rows, rows, wide, rows, rows, wide, rows, rows, rows, wide, rows, rows, rows,
        wide, rows,
    )
    return jax.shard_map(
        shards, mesh=mesh, in_specs=placed, out_specs=wide, check_vma=False
    )
```

time: 80.2 us -> 68.4 us (0.85)
  Pallas kernels: 77.3 us -> 65.4 us
    pallas_call x1, Pallas kernels: 77.3 us -> 65.4 us  [shards(): pl.pallas_call(kernel, out_shape=jax.ShapeDtypeStruct((GROUPS_DEV, D), F3...]
where the time goes in v3:
time: 68.4 us; the launch traced here: 68.1 us
  Pallas kernels  65.4 us (96%)
  local copies, waits for them, and re-layouts  1.38 us (2%)
  between operations  1.3 us (2%)
    pallas_call x1, Pallas kernels, shards(): pl.pallas_call(kernel, out_shape=jax.ShapeDtypeStruct((GROUPS_DEV, D), F3...  65.4 us
    unnamed x1, local copies, waits for them, and re-layouts  1.38 us

profile of v3, /device:TPU:1, one launch (start us, length us, event | category | flops | bytes accessed | tf_op | source)
XLA Modules:
  0.0 68.1 jit_solution(8839939334205526290)
XLA Ops:
  1.3 65.4 %shard_map.163 = f32[32,256]{1,0:T(8,128)} custom-call(s32[128,128]{1,0:T(8,128)} %bitcast.11, s32[8,128]{1,0:T(8,128)} %bitcast.17, s32[8,128]{1,0:T(8,128)} %bitcast.18, s32[8,128]{1,0:T(8,128)} %bitcast.19, s32[8,128]{1,0:T(8,128)} %bitcast.20, s32[8,128]{1,0:T(8,128)} %bitcast.21, s32[32,128]{1,0:T(8,128)} %bitcast.12, s32[32,128]{1,0:T(8,128)} %bitcast.13, ...), custom_call_target="tpu_custom_call" | custom-call | tf_op jit(solution)/shard_map/pallas_call | solution.py:538
  66.8 1.4 %copy.21 = f32[32,256]{1,0:T(8,128)} copy(f32[32,256]{1,0:T(8,128)} %shard_map.163) | data formatting | bytes 65536

commit v4 on v3

--- a/solution.py
+++ b/solution.py
@@ -19,7 +19,9 @@
 PEERS = 64
 HALF = 2048
 OWNER_STEP = 11
-CHUNK = 512
+CHUNK, SMALL = 512, 256
+CHUNKS = [(0, 256), (256, 512), (768, 512), (1280, 512), (1792, 256)]
+EARLY = 3
 
 
 def apart(code):
@@ -102,33 +104,35 @@
 
 
 def kernel(
-    key_slot, da_key, da_group, da_mult, db_key, db_mult, b_slot, b_weight, a_slot, a_weight,
-    a_group, da_count_hbm, db_count_hbm, da_hbm, db_hbm, b_hbm, a_hbm,
+    key_slot_hbm, db_key_hbm, db_mult_hbm, db_count_hbm, db_hbm, b_slot_hbm, b_weight_hbm, b_hbm,
+    da_key_hbm, da_group_hbm, da_mult_hbm, da_count_hbm, da_hbm, a_slot_hbm, a_weight_hbm,
+    a_group_hbm, a_hbm,
     out,
-    da_count, db_count, da_rows, db_rows, b_rows, a_rows, spot_ref, sign_ref,
+    key_slot, db_key, db_mult, b_slot, b_weight, da_key, da_group, da_mult, a_slot, a_weight,
+    a_group, da_count, db_count, da_rows, db_rows, b_rows, a_rows, spot_ref, sign_ref,
     db_send, da_send, db_info, da_info, db_recv, da_recv, db_info_recv, da_info_recv,
     part_b, quarter_b, got_b, full_b, part_db, quarter_db, got_db, full_db,
-    pick, pick_d, table_a, table_w, terms, spots, near_send, near_recv, far_send, far_recv, own, total_ref,
-    load_sems, sems, near_sems, planes,
+    pick, pick_d, table_a, table_w, terms, spots, near_send, near_recv, far_send, far_recv, own, big_sum, small_sum, early,
+    load_sems, sems, near_sems, part_sems, planes,
 ):
     k, x = lax.axis_index("keys"), lax.axis_index("view")
     core = lax.rem(k, 2)
     partner = k + 1 - 2 * core
     y, z = k // 8, lax.rem(k // 2, 4)
 
-    def load(src, dst, s):
-        return pltpu.make_async_copy(src, dst, load_sems.at[s])
-
+    pairs = (
+        (key_slot_hbm, key_slot), (db_key_hbm, db_key), (db_mult_hbm, db_mult),
+        (db_count_hbm, db_count), (db_hbm, db_rows), (b_slot_hbm, b_slot),
+        (b_weight_hbm, b_weight), (b_hbm, b_rows), (da_key_hbm, da_key),
+        (da_group_hbm, da_group), (da_mult_hbm, da_mult), (da_count_hbm, da_count),
+        (da_hbm, da_rows), (a_slot_hbm, a_slot), (a_weight_hbm, a_weight),
+        (a_group_hbm, a_group), (a_hbm, a_rows),
+    )
     loads = [
-        load(db_hbm, db_rows, 0),
-        load(da_hbm, da_rows, 1),
-        load(b_hbm, b_rows, 2),
-        load(a_hbm, a_rows, 3),
-        load(da_count_hbm, da_count, 4),
-        load(db_count_hbm, db_count, 5),
+        pltpu.make_async_copy(src, dst, load_sems.at[n]) for n, (src, dst) in enumerate(pairs)
     ]
-    loads[5].start()
-    loads[0].start()
+    for n in range(4):
+        loads[n].start()
 
     def peer(code):
         to_y, to_z = lax.rem(y + (code >> 4), 4), lax.rem(z + ((code >> 2) & 3), 4)
@@ -152,10 +156,12 @@
         for j in range(1, VIEWS):
             to = {"keys": k, "view": lax.rem(x + j, VIEWS)}
             pl.semaphore_signal(barrier, inc=1, device_id=to, device_id_type=MESH)
-        for n in (4, 1, 2, 3):
+        for n in range(4, len(loads)):
             loads[n].start()
 
     with jax.named_scope("lookup_b"):
+        for n in range(4):
+            loads[n].wait()
         whole = key_slot[...]
         high = (whole >> 7).astype(F32).T
         low = (whole & 127).astype(F32).T
@@ -168,7 +174,6 @@
                 sign_ref[8 * r + s : 8 * r + s + 1, :] = mult_ref[s : s + 1, :].astype(F32)
             return slots, marks, ranks
 
-        loads[5].wait()
         slots_b, marks_b, ranks_b = look_up(0, db_key, db_mult, db_count)
         note = by_place(
             marks_b, ranks_b, [[v >> 4 for v in slots_b], [v & 15 for v in slots_b]]
@@ -198,7 +203,7 @@
             picks.append(jnp.concatenate(parts, axis=1))
         return dot(jnp.concatenate(picks, axis=0), rows[...]).astype(BF16)
 
-    loads[0].wait()
+    loads[4].wait()
 
     def pack_b(i, carry):
         blocks = packed(0, i, db_rows)
@@ -235,6 +240,9 @@
     db_recv[0, 0] = db_send[0, 0]
     db_recv[1, 0] = db_send[1, 0]
 
+    def eighth(at, part):
+        return pl.ds(pl.multiple_of(at * 128 + part * 64, 64), 64)
+
     def quarter(at):
         return pl.ds(pl.multiple_of(at * 128, 128), 128)
 
@@ -253,7 +261,8 @@
                 mine, full.at[quarter(x)], sems.at[s], sems.at[s + 1], {"keys": k, "view": to}
             ).start()
 
-    loads[2].wait()
+    for n in (5, 6, 7):
+        loads[n].wait()
     with jax.named_scope("sum_b"):
         for m in range(2):
             acc = jnp.zeros((256, D), F32)
@@ -266,7 +275,8 @@
         across(part_b, got_b, 8)
 
     with jax.named_scope("lookup_a"):
-        loads[4].wait()
+        for n in range(8, 12):
+            loads[n].wait()
         slots_a, marks_a, ranks_a = look_up(1, da_key, da_mult, da_count)
         groups = [da_group[s : s + 1, :] for s in range(8)]
         note = by_place(
@@ -283,7 +293,7 @@
         group_note = (note[2 * OWNERS : 3 * OWNERS] * 64.0 + note[3 * OWNERS :]).astype(I32)
         for n in range(OWNERS):
             da_info[n] = jnp.concatenate([slot_note[n : n + 1, :], group_note[n : n + 1, :]], axis=0)
-    loads[1].wait()
+    loads[12].wait()
 
     def pack_a(i, carry):
         blocks = packed(1, i, da_rows)
@@ -321,20 +331,6 @@
         quarter_db[h] = part_db[h, quarter(x), :] + got_db[h, 0] + got_db[h, 1] + got_db[h, 2]
         all_quarters(quarter_db.at[h], full_db.at[h], 16 + 4 * h)
         full_db[h, quarter(x), :] = quarter_db[h]
-
-    with jax.named_scope("wait_db0"):
-        wait_bytes(db_info_recv.at[1:OWNERS], sems.at[1])
-        wait_bytes(db_recv.at[0, 1:OWNERS], sems.at[3])
-    sum_db(0)
-    across(part_db.at[0], got_db.at[0], 14)
-
-    with jax.named_scope("wait_b"):
-        wait_bytes(got_b, sems.at[9])
-    whole_b = part_b[quarter(x), :] + got_b[0] + got_b[1] + got_b[2]
-    for h in range(2):
-        quarter_b[h] = whole_b[:, h * LANES : (h + 1) * LANES]
-        full_b[h, quarter(x), :] = quarter_b[h]
-    all_quarters(quarter_b.at[0], full_b.at[0], 10)
 
     at_lane = iota((LANES, LANES), 1)
 
@@ -349,6 +345,8 @@
             ).astype(BF16)
         return carry
 
+    for n in (13, 14, 15):
+        loads[n].wait()
     with jax.named_scope("pick"):
         lax.fori_loop(0, 32, pick_block, 0)
 
@@ -363,21 +361,41 @@
 
     spots[0:32, :] = place(a_group[...])
 
+    with jax.named_scope("wait_db0"):
+        wait_bytes(db_info_recv.at[1:OWNERS], sems.at[1])
+        wait_bytes(db_recv.at[0, 1:OWNERS], sems.at[3])
+    sum_db(0)
+    across(part_db.at[0], got_db.at[0], 14)
+
+    with jax.named_scope("wait_b"):
+        wait_bytes(got_b, sems.at[9])
+    whole_b = part_b[quarter(x), :] + got_b[0] + got_b[1] + got_b[2]
+    for h in range(2):
+        quarter_b[h] = whole_b[:, h * LANES : (h + 1) * LANES]
+        full_b[h, quarter(x), :] = quarter_b[h]
+    all_quarters(quarter_b.at[0], full_b.at[0], 10)
+
+    with jax.named_scope("wait_db1"):
+        wait_bytes(db_recv.at[1, 1:OWNERS], sems.at[5])
+    def send_a(n, carry):
+        to = {"keys": owner_of(n), "view": x}
+        send(da_send.at[n], da_recv.at[home(n)], sems.at[12], sems.at[13], to).start()
+        return carry
+
+    lax.fori_loop(1, OWNERS, send_a, 0)
+
+    sum_db(1)
+    for part in range(2):
+        for j in range(1, VIEWS):
+            to = lax.rem(x + j, VIEWS)
+            send(
+                part_db.at[1, eighth(to, part)], got_db.at[1, j - 1, 64 * part : 64 * part + 64],
+                part_sems.at[part, 0], part_sems.at[part, 1], {"keys": k, "view": to},
+            ).start()
+
     with jax.named_scope("wait_rs0"):
         wait_bytes(got_db.at[0], sems.at[15])
     finish_quarter(0)
-
-    with jax.named_scope("wait_db1"):
-        wait_bytes(db_recv.at[1, 1:OWNERS], sems.at[5])
-    sum_db(1)
-    across(part_db.at[1], got_db.at[1], 18)
-
-    def send_a(n, carry):
-        to = {"keys": owner_of(n), "view": x}
-        send(da_send.at[n], da_recv.at[home(n)], sems.at[12], sems.at[13], to).start()
-        return carry
-
-    lax.fori_loop(1, OWNERS, send_a, 0)
 
     with jax.named_scope("wait_da_info"):
         wait_bytes(da_info_recv.at[1:OWNERS], sems.at[7])
@@ -401,21 +419,35 @@
         table_a[h] = split(full_db[h])
 
         def block(j, carry):
-            at = pl.ds(pl.multiple_of(j * 1024, 1024), 1024)
+            at = pl.ds(pl.multiple_of(j * 2048, 2048), 2048)
             cut = slice(h * LANES, (h + 1) * LANES)
             both = dot(pick[at, :], table_a[h])
             value = (both[:, :LANES] + both[:, LANES:]) * a_rows[at, cut].astype(F32)
             terms[at, cut] = value.astype(BF16)
             return carry
 
-        lax.fori_loop(0, 4, block, 0)
-
-    with jax.named_scope("wait_rs1"):
-        wait_bytes(got_db.at[1], sems.at[19])
-    finish_quarter(1)
+        lax.fori_loop(0, 2, block, 0)
+
+    for part in range(2):
+        cut = slice(64 * part, 64 * part + 64)
+        with jax.named_scope("wait_rs1"):
+            wait_bytes(got_db.at[1, :, cut], part_sems.at[part, 1])
+        quarter_db[1, cut] = (
+            part_db[1, eighth(x, part), :]
+            + got_db[1, 0, cut]
+            + got_db[1, 1, cut]
+            + got_db[1, 2, cut]
+        )
+        for j in range(1, VIEWS):
+            to = lax.rem(x + j, VIEWS)
+            send(
+                quarter_db.at[1, cut], full_db.at[1, eighth(x, part)], sems.at[20], sems.at[21],
+                {"keys": k, "view": to},
+            ).start()
+        full_db[1, eighth(x, part), :] = quarter_db[1, cut]
     all_quarters(quarter_b.at[1], full_b.at[1], 24)
 
-    loads[3].wait()
+    loads[16].wait()
     with jax.named_scope("wait_ag0"):
         wait_bytes(full_db.at[0, 0:384], sems.at[17])
     with jax.named_scope("a_terms0"):
@@ -425,6 +457,30 @@
         wait_bytes(full_db.at[1, 0:384], sems.at[21])
     with jax.named_scope("a_terms1"):
         a_terms(1)
+
+    def base_of(t, steps):
+        base = 0
+        for n, (other, c) in enumerate(steps):
+            base = jnp.where(t == n, other * HALF + CHUNKS[c][0], base)
+        return base
+
+    def summed(base, height, first, last):
+        acc = jnp.zeros((height, D), F32)
+        for p in range(first, last):
+            rows = [spots[4 * p + s : 4 * p + s + 1, :] for s in range(4)]
+            acc = acc + dot(one_hot(rows, height, base), terms[512 * p : 512 * (p + 1), :])
+        return acc
+
+    last = len(CHUNKS) - 1
+    small_steps = [(1, 0), (1, last), (0, 0), (0, last)]
+    big_steps = [(other, c) for c in range(1, last) for other in (1, 0)]
+
+    def early_step(t, carry):
+        early[t] = summed(base_of(t, small_steps), SMALL, 0, 8)
+        return carry
+
+    with jax.named_scope("early"):
+        lax.fori_loop(0, EARLY, early_step, 0)
 
     with jax.named_scope("wait_ag_b"):
         wait_bytes(full_b.at[0, 0:384], sems.at[11])
@@ -449,53 +505,56 @@
     with jax.named_scope("d_terms"):
         lax.fori_loop(0, 4, d_block, 0)
 
-    def summed(base):
-        acc = jnp.zeros((CHUNK, D), F32)
-        for p in range(12):
-            rows = [spots[4 * p + s : 4 * p + s + 1, :] for s in range(4)]
-            acc = acc + dot(one_hot(rows, CHUNK, base), terms[512 * p : 512 * (p + 1), :])
-        return acc
-
-    chunks = HALF // CHUNK
-    blocks_each = CHUNK // GROUPS_DEV
-    steps = [(other, c) for c in range(chunks) for other in (1, 0)]
-
-    def group_step(t, carry):
-        base = 0
-        for n, (other, c) in enumerate(steps):
-            base = jnp.where(t == n, other * HALF + c * CHUNK, base)
-        total_ref[...] = summed(base)
-        for n, (other, c) in enumerate(steps):
+    def finish_step(t, some, held_sum):
+        for n, other, c in some:
+            start, size = CHUNKS[c]
 
             @pl.when(t == n)
-            def _(other=other, c=c):
+            def _(other=other, c=c, start=start, size=size):
+                rows = slice(start, start + size)
                 if other:
-                    near_send[c] = total_ref[...]
+                    near_send[rows] = held_sum[...]
                     send(
-                        near_send.at[c], near_recv.at[c], near_sems.at[0, c], near_sems.at[1, c],
-                        {"keys": partner, "view": x},
+                        near_send.at[rows], near_recv.at[rows], near_sems.at[0, c],
+                        near_sems.at[1, c], {"keys": partner, "view": x},
                     ).start()
                     return
-                wait_bytes(near_recv.at[c], near_sems.at[1, c])
-                acc = total_ref[...] + near_recv[c]
-                if c + 1 == chunks:
-                    own[...] = acc[CHUNK - GROUPS_DEV :, :]
-                far_send[c * blocks_each : (c + 1) * blocks_each] = acc.astype(BF16).reshape(
-                    blocks_each, GROUPS_DEV, D
-                )
+                wait_bytes(near_recv.at[rows], near_sems.at[1, c])
+                acc = held_sum[...] + near_recv[rows]
+                if c == last:
+                    own[...] = acc[size - GROUPS_DEV :, :]
+                blocks = slice(start // GROUPS_DEV, (start + size) // GROUPS_DEV)
+                far_send[blocks] = acc.astype(BF16).reshape(size // GROUPS_DEV, GROUPS_DEV, D)
                 if c == 0:
                     pl.semaphore_wait(planes, VIEWS - 1)
-                for m in range(c * blocks_each, (c + 1) * blocks_each):
+                for m in range(blocks.start, blocks.stop):
                     code = FAR_FIRST[m]
                     if code:
                         send(
                             far_send.at[m], far_recv.at[code], sems.at[22], sems.at[23], peer(code)
                         ).start()
 
-        return carry
-
+    def begun_step(t, carry):
+        small_sum[...] = early[t] + summed(base_of(t, small_steps), SMALL, 8, 12)
+        finish_step(t, [(n, *small_steps[n]) for n in range(EARLY)], small_sum)
+        return carry
+
+    def big_step(t, carry):
+        big_sum[...] = summed(base_of(t, big_steps), CHUNK, 0, 12)
+        finish_step(t, [(n, *step) for n, step in enumerate(big_steps)], big_sum)
+        return carry
+
+    def last_step(t, carry):
+        small_sum[...] = summed(base_of(t, small_steps), SMALL, 0, 12)
+        finish_step(t, [(n, *small_steps[n]) for n in range(EARLY, 4)], small_sum)
+        return carry
+
+    with jax.named_scope("begun"):
+        lax.fori_loop(0, EARLY, begun_step, 0)
     with jax.named_scope("groups"):
-        lax.fori_loop(0, len(steps), group_step, 0)
+        lax.fori_loop(0, len(big_steps), big_step, 0)
+    with jax.named_scope("last"):
+        lax.fori_loop(EARLY, 4, last_step, 0)
 
     with jax.named_scope("wait_far"):
         wait_bytes(far_recv.at[1:PEERS], sems.at[23])
@@ -514,11 +573,12 @@
     wait_bytes(full_b.at[1, 0:384], sems.at[24])
     wait_bytes(da_send.at[1:OWNERS], sems.at[12])
     for h in range(2):
-        wait_bytes(part_db.at[h, 0:384], sems.at[14 + 4 * h])
         wait_bytes(part_db.at[h, 0:384], sems.at[16 + 4 * h])
+        wait_bytes(got_db.at[1, :, 0:64], part_sems.at[h, 0])
+    wait_bytes(part_db.at[0, 0:384], sems.at[14])
     wait_bytes(far_send.at[0 : PEERS - 1], sems.at[22])
-    for c in range(chunks):
-        wait_bytes(near_send.at[c], near_sems.at[0, c])
+    for c, (start, size) in enumerate(CHUNKS):
+        wait_bytes(near_send.at[start : start + size], near_sems.at[0, c])
 
 
 def shards(
@@ -527,7 +587,6 @@
 ):
     vmem = pl.BlockSpec(memory_space=pltpu.VMEM)
     hbm = pl.BlockSpec(memory_space=pl.ANY)
-    fixed = pl.BlockSpec(memory_space=pltpu.HBM)
 
     def lanes(v):
         return v.reshape(-1, LANES)
@@ -538,9 +597,20 @@
     return pl.pallas_call(
         kernel,
         out_shape=jax.ShapeDtypeStruct((GROUPS_DEV, D), F32),
-        in_specs=[vmem] * 11 + [fixed] * 2 + [hbm] * 4,
+        in_specs=[hbm] * 17,
         out_specs=vmem,
         scratch_shapes=[
+            held(LANES, LANES, dtype=I32),
+            held(8, LANES, dtype=I32),
+            held(8, LANES, dtype=I32),
+            held(32, LANES, dtype=I32),
+            held(32, LANES, dtype=I32),
+            held(8, LANES, dtype=I32),
+            held(8, LANES, dtype=I32),
+            held(8, LANES, dtype=I32),
+            held(32, LANES, dtype=I32),
+            held(32, LANES, dtype=I32),
+            held(32, LANES, dtype=I32),
             pltpu.SMEM((1,), I32),
             pltpu.SMEM((1,), I32),
             held(DELTA, D, dtype=BF16),
@@ -571,24 +641,27 @@
             held(2, KEYS_DEV, D, dtype=BF16),
             held(ROWS + OWNERS * CAP, D, dtype=BF16),
             held(48, LANES, dtype=I32),
-            held(HALF // CHUNK, CHUNK, D),
-            held(HALF // CHUNK, CHUNK, D),
+            held(HALF, D),
+            held(HALF, D),
             held(PEERS, GROUPS_DEV, D, dtype=BF16),
             held(PEERS, GROUPS_DEV, D, dtype=BF16),
             held(GROUPS_DEV, D),
             held(CHUNK, D),
-            pltpu.SemaphoreType.DMA((6,)),
+            held(SMALL, D),
+            held(EARLY, SMALL, D),
+            pltpu.SemaphoreType.DMA((17,)),
             pltpu.SemaphoreType.DMA((26,)),
-            pltpu.SemaphoreType.DMA((2, HALF // CHUNK)),
+            pltpu.SemaphoreType.DMA((2, len(CHUNKS))),
+            pltpu.SemaphoreType.DMA((2, 2)),
             pltpu.SemaphoreType.REGULAR,
         ],
         compiler_params=pltpu.CompilerParams(
             collective_id=0, has_side_effects=True, vmem_limit_bytes=56 * 1024 * 1024
         ),
     )(
-        lanes(key_slot), lanes(da_key), lanes(da_group), lanes(da_mult), lanes(db_key),
-        lanes(db_mult), lanes(b_slot), lanes(b_weight), lanes(a_slot), lanes(a_weight),
-        lanes(a_group), da_count, db_count, da_payload, db_payload, b_payload, a_payload,
+        lanes(key_slot), lanes(db_key), lanes(db_mult), db_count, db_payload, lanes(b_slot),
+        lanes(b_weight), b_payload, lanes(da_key), lanes(da_group), lanes(da_mult), da_count,
+        da_payload, lanes(a_slot), lanes(a_weight), lanes(a_group), a_payload,
     )
 
 

time: 68.4 us -> 65.9 us (0.963)
  Pallas kernels: 65.4 us -> 63 us
    pallas_call x1, Pallas kernels: 65.4 us -> 63 us  [shards(): pl.pallas_call(kernel, out_shape=jax.ShapeDtypeStruct((GROUPS_DEV, D), F3...]
where the time goes in v4:
time: 65.9 us; the launch traced here: 65.7 us
  Pallas kernels  63 us (96%)
  local copies, waits for them, and re-layouts  1.38 us (2%)
  between operations  1.3 us (2%)
    pallas_call x1, Pallas kernels, shards(): pl.pallas_call(kernel, out_shape=jax.ShapeDtypeStruct((GROUPS_DEV, D), F3...  63 us
    unnamed x1, local copies, waits for them, and re-layouts  1.38 us

profile of v4, /device:TPU:1, one launch (start us, length us, event | category | flops | bytes accessed | tf_op | source)
XLA Modules:
  0.0 65.7 jit_solution(1538504115080308813)
XLA Ops:
  1.3 63.0 %shard_map.163 = f32[32,256]{1,0:T(8,128)} custom-call(s32[128,128]{1,0:T(8,128)} %bitcast.11, s32[8,128]{1,0:T(8,128)} %bitcast.17, s32[8,128]{1,0:T(8,128)} %bitcast.18, s32[1]{0:T(128)S(6)} %copy.20.db_count_hbm, bf16[1024,256]{1,0:T(8,128)(2,1)} %db_hbm.1, s32[32,128]{1,0:T(8,128)} %bitcast.12, s32[32,128]{1,0:T(8,128)} %bitcast.13, ...), custom_call_target="tpu_custom_call" | custom-call | tf_op jit(solution)/shard_map/pallas_call | solution.py:597
  64.3 1.4 %copy.21 = f32[32,256]{1,0:T(8,128)} copy(f32[32,256]{1,0:T(8,128)} %shard_map.163) | data formatting | bytes 65536

commit v5 on v4

--- a/solution.py
+++ b/solution.py
@@ -18,10 +18,7 @@
 LANES = 128
 PEERS = 64
 HALF = 2048
-OWNER_STEP = 11
-CHUNK, SMALL = 512, 256
-CHUNKS = [(0, 256), (256, 512), (768, 512), (1280, 512), (1792, 256)]
-EARLY = 3
+CHUNK = 512
 
 
 def apart(code):
@@ -29,6 +26,7 @@
 
 
 FAR_FIRST = sorted(range(PEERS), key=lambda code: (-apart(code), (code * 27) % PEERS))
+OWNERS_MIXED = [11 * n % OWNERS for n in range(1, OWNERS)]
 RANK = [FAR_FIRST.index(code) for code in range(PEERS)]
 
 
@@ -112,8 +110,9 @@
     a_group, da_count, db_count, da_rows, db_rows, b_rows, a_rows, spot_ref, sign_ref,
     db_send, da_send, db_info, da_info, db_recv, da_recv, db_info_recv, da_info_recv,
     part_b, quarter_b, got_b, full_b, part_db, quarter_db, got_db, full_db,
-    pick, pick_d, table_a, table_w, terms, spots, near_send, near_recv, far_send, far_recv, own, big_sum, small_sum, early,
-    load_sems, sems, near_sems, part_sems, planes,
+    pick, pick_d, table_a, table_w, terms, spots, near_send, near_recv, far_send, far_recv, own, chunk_sum, part_sum,
+    spot_cols, a_turned, a_term,
+    load_sems, sems, near_sems, part_sems, far_sems, planes,
 ):
     k, x = lax.axis_index("keys"), lax.axis_index("view")
     core = lax.rem(k, 2)
@@ -182,35 +181,21 @@
         for n in range(OWNERS):
             db_info[n] = note[n : n + 1, :]
 
-    def home(i):
-        return lax.rem(OWNER_STEP * i, OWNERS)
-
-    def owner_of(i):
-        code = home(i)
-        to_y, to_z = lax.rem(y + code // 8, 4), lax.rem(z + lax.rem(code // 2, 4), 4)
-        return (to_y * 4 + to_z) * 2 + lax.rem(core + lax.rem(code, 2), 2)
+    def owner_of(code):
+        to_y, to_z = lax.rem(y + code // 8, 4), lax.rem(z + (code // 2) % 4, 4)
+        return (to_y * 4 + to_z) * 2 + lax.rem(core + code % 2, 2)
 
     def packed(r, i, rows):
-        at = iota((CAP, LANES), 0)
-        picks = []
-        for q in range(8):
-            base = owner_of(8 * i + q) * CAP
-            parts = []
-            for s in range(8):
-                spot = spot_ref[8 * r + s : 8 * r + s + 1, :]
-                sign = sign_ref[8 * r + s : 8 * r + s + 1, :]
-                parts.append(jnp.where(at == spot - base, sign, 0.0).astype(BF16))
-            picks.append(jnp.concatenate(parts, axis=1))
-        return dot(jnp.concatenate(picks, axis=0), rows[...]).astype(BF16)
+        spots = [spot_ref[8 * r + s : 8 * r + s + 1, :] for s in range(8)]
+        signs = [sign_ref[8 * r + s : 8 * r + s + 1, :] for s in range(8)]
+        return dot(one_hot(spots, 512, 512 * i, signs), rows[...]).astype(BF16)
 
     loads[4].wait()
 
     def pack_b(i, carry):
-        blocks = packed(0, i, db_rows)
-        for q in range(8):
-            n = 8 * i + q
-            for h in range(2):
-                db_send[h, n] = blocks[q * CAP : (q + 1) * CAP, h * LANES : (h + 1) * LANES]
+        blocks = packed(0, i, db_rows).reshape(8, CAP, D)
+        for h in range(2):
+            db_send[h, pl.ds(8 * i, 8)] = blocks[:, :, h * LANES : (h + 1) * LANES]
         return carry
 
     with jax.named_scope("pack_b"):
@@ -219,26 +204,22 @@
     with jax.named_scope("barrier"):
         pl.semaphore_wait(barrier, OWNERS - 1 + VIEWS - 1)
 
-    def first_half(n, carry):
-        to = {"keys": owner_of(n), "view": x}
-        send(db_info.at[owner_of(n)], db_info_recv.at[home(n)], sems.at[0], sems.at[1], to).start()
-        send(db_send.at[0, n], db_recv.at[0, home(n)], sems.at[2], sems.at[3], to).start()
-        return carry
-
-    def second_half(n, carry):
-        to = {"keys": owner_of(n), "view": x}
-        send(db_send.at[1, n], db_recv.at[1, home(n)], sems.at[4], sems.at[5], to).start()
-        return carry
-
     with jax.named_scope("send_b"):
-        lax.fori_loop(1, OWNERS, first_half, 0)
+        for code in OWNERS_MIXED:
+            n = owner_of(code)
+            to = {"keys": n, "view": x}
+            send(db_info.at[n], db_info_recv.at[code], sems.at[0], sems.at[1], to).start()
+            send(db_send.at[0, n], db_recv.at[0, code], sems.at[2], sems.at[3], to).start()
+        for code in OWNERS_MIXED:
+            n = owner_of(code)
+            to = {"keys": n, "view": x}
+            send(db_send.at[1, n], db_recv.at[1, code], sems.at[4], sems.at[5], to).start()
         for j in range(1, VIEWS):
             to = {"keys": k, "view": lax.rem(x + j, VIEWS)}
             pl.semaphore_signal(planes, inc=1, device_id=to, device_id_type=MESH)
-        lax.fori_loop(1, OWNERS, second_half, 0)
     db_info_recv[0] = db_info[k]
-    db_recv[0, 0] = db_send[0, 0]
-    db_recv[1, 0] = db_send[1, 0]
+    db_recv[0, 0] = db_send[0, k]
+    db_recv[1, 0] = db_send[1, k]
 
     def eighth(at, part):
         return pl.ds(pl.multiple_of(at * 128 + part * 64, 64), 64)
@@ -296,22 +277,18 @@
     loads[12].wait()
 
     def pack_a(i, carry):
-        blocks = packed(1, i, da_rows)
-        for q in range(8):
-            da_send[8 * i + q] = blocks[q * CAP : (q + 1) * CAP, :]
+        da_send[pl.ds(8 * i, 8)] = packed(1, i, da_rows).reshape(8, CAP, D)
         return carry
 
     with jax.named_scope("pack_a"):
         lax.fori_loop(0, 4, pack_a, 0)
 
-    def send_a_info(n, carry):
-        to = {"keys": owner_of(n), "view": x}
-        send(da_info.at[owner_of(n)], da_info_recv.at[home(n)], sems.at[6], sems.at[7], to).start()
-        return carry
-
-    lax.fori_loop(1, OWNERS, send_a_info, 0)
+    for code in OWNERS_MIXED:
+        n = owner_of(code)
+        to = {"keys": n, "view": x}
+        send(da_info.at[n], da_info_recv.at[code], sems.at[6], sems.at[7], to).start()
     da_info_recv[0] = da_info[k]
-    da_recv[0] = da_send[0]
+    da_recv[0] = da_send[k]
 
     left = iota((1, LANES), 1) < CAP
 
@@ -334,22 +311,6 @@
 
     at_lane = iota((LANES, LANES), 1)
 
-    def pick_block(j, carry):
-        row = a_slot[pl.ds(j, 1), :] + KEYS_DEV * a_weight[pl.ds(j, 1), :]
-        cols = jnp.broadcast_to(row.astype(F32), (LANES, LANES)).T.astype(I32)
-        slot, weight = cols & (KEYS_DEV - 1), (cols >> 9).astype(F32)
-        at = pl.ds(pl.multiple_of(j * LANES, LANES), LANES)
-        for q in range(4):
-            pick[at, q * LANES : (q + 1) * LANES] = jnp.where(
-                at_lane + q * LANES == slot, weight, 0.0
-            ).astype(BF16)
-        return carry
-
-    for n in (13, 14, 15):
-        loads[n].wait()
-    with jax.named_scope("pick"):
-        lax.fori_loop(0, 32, pick_block, 0)
-
     def place(group):
         to_y, to_z, to_x = group >> 10, (group >> 8) & 3, (group >> 5) & 3
         code = ((to_y - y) & 3) * 16 + ((to_z - z) & 3) * 4 + ((to_x - x) & 3)
@@ -359,7 +320,23 @@
         other = ((group >> 7) & 1) ^ core
         return other * HALF + rank * GROUPS_DEV + (group & 31)
 
-    spots[0:32, :] = place(a_group[...])
+    for n in range(13, 17):
+        loads[n].wait()
+    with jax.named_scope("pick"):
+        spots[0:32, :] = place(a_group[...])
+
+        def pick_block(j, carry):
+            at = pl.ds(pl.multiple_of(j * LANES, LANES), LANES)
+            value = a_weight[pl.ds(j, 1), :].astype(F32)
+            pick[:, at] = one_hot([a_slot[pl.ds(j, 1), :]], KEYS_DEV, 0, [value])
+            row = jnp.broadcast_to(spots[pl.ds(j, 1), :].astype(F32), (LANES, LANES))
+            spot_cols[at, :] = row.T.astype(I32) - at_lane
+            turned = a_rows[at, :].astype(F32).T.astype(BF16)
+            for h in range(2):
+                a_turned[h, :, at] = turned[h * LANES : (h + 1) * LANES, :]
+            return carry
+
+        lax.fori_loop(0, 32, pick_block, 0)
 
     with jax.named_scope("wait_db0"):
         wait_bytes(db_info_recv.at[1:OWNERS], sems.at[1])
@@ -373,17 +350,13 @@
     for h in range(2):
         quarter_b[h] = whole_b[:, h * LANES : (h + 1) * LANES]
         full_b[h, quarter(x), :] = quarter_b[h]
-    all_quarters(quarter_b.at[0], full_b.at[0], 10)
 
     with jax.named_scope("wait_db1"):
         wait_bytes(db_recv.at[1, 1:OWNERS], sems.at[5])
-    def send_a(n, carry):
-        to = {"keys": owner_of(n), "view": x}
-        send(da_send.at[n], da_recv.at[home(n)], sems.at[12], sems.at[13], to).start()
-        return carry
-
-    lax.fori_loop(1, OWNERS, send_a, 0)
-
+    for code in OWNERS_MIXED:
+        n = owner_of(code)
+        to = {"keys": n, "view": x}
+        send(da_send.at[n], da_recv.at[code], sems.at[12], sems.at[13], to).start()
     sum_db(1)
     for part in range(2):
         for j in range(1, VIEWS):
@@ -396,6 +369,7 @@
     with jax.named_scope("wait_rs0"):
         wait_bytes(got_db.at[0], sems.at[15])
     finish_quarter(0)
+
 
     with jax.named_scope("wait_da_info"):
         wait_bytes(da_info_recv.at[1:OWNERS], sems.at[7])
@@ -416,17 +390,47 @@
         return jnp.concatenate([top, (value - top.astype(F32)).astype(BF16)], axis=1)
 
     def a_terms(h):
-        table_a[h] = split(full_db[h])
+        flat = full_db[h].T
+        top = flat.astype(BF16)
+        table_a[...] = jnp.concatenate([top, (flat - top.astype(F32)).astype(BF16)], axis=0)
 
         def block(j, carry):
             at = pl.ds(pl.multiple_of(j * 2048, 2048), 2048)
-            cut = slice(h * LANES, (h + 1) * LANES)
-            both = dot(pick[at, :], table_a[h])
-            value = (both[:, :LANES] + both[:, LANES:]) * a_rows[at, cut].astype(F32)
-            terms[at, cut] = value.astype(BF16)
+            both = dot(table_a[...], pick[:, at])
+            value = (both[:LANES] + both[LANES:]) * a_turned[h, :, at].astype(F32)
+            a_term[h, :, at] = value.astype(BF16)
             return carry
 
         lax.fori_loop(0, 2, block, 0)
+
+    def pick_base(t, bases):
+        base = 0
+        for n, value in enumerate(bases):
+            base = jnp.where(t == n, value, base)
+        return base
+
+    def a_sum(h, base, width):
+        acc = jnp.zeros((LANES, width), F32)
+        for p in range(16):
+            at = slice(256 * p, 256 * (p + 1))
+            cols = spot_cols[at, :] - base
+            hits = jnp.concatenate(
+                [
+                    jnp.where(cols == q * LANES, 1.0, 0.0).astype(BF16)
+                    for q in range(width // LANES)
+                ],
+                axis=1,
+            )
+            acc = acc + dot(a_term[h, :, at], hits)
+        return acc.T
+
+    def a_sums(h, bases, width=1024):
+        def block(t, carry):
+            base = pl.multiple_of(pick_base(t, bases), width)
+            part_sum[pl.ds(base, width), h * LANES : (h + 1) * LANES] = a_sum(h, base, width)
+            return carry
+
+        lax.fori_loop(0, len(bases), block, 0)
 
     for part in range(2):
         cut = slice(64 * part, 64 * part + 64)
@@ -445,42 +449,21 @@
                 {"keys": k, "view": to},
             ).start()
         full_db[1, eighth(x, part), :] = quarter_db[1, cut]
-    all_quarters(quarter_b.at[1], full_b.at[1], 24)
-
-    loads[16].wait()
+
+    for h in range(2):
+        all_quarters(quarter_b.at[h], full_b.at[h], 10 + 14 * h)
     with jax.named_scope("wait_ag0"):
         wait_bytes(full_db.at[0, 0:384], sems.at[17])
     with jax.named_scope("a_terms0"):
         a_terms(0)
-
+    with jax.named_scope("a_sums0b"):
+        a_sums(0, [HALF, 0])
     with jax.named_scope("wait_ag1"):
         wait_bytes(full_db.at[1, 0:384], sems.at[21])
     with jax.named_scope("a_terms1"):
         a_terms(1)
-
-    def base_of(t, steps):
-        base = 0
-        for n, (other, c) in enumerate(steps):
-            base = jnp.where(t == n, other * HALF + CHUNKS[c][0], base)
-        return base
-
-    def summed(base, height, first, last):
-        acc = jnp.zeros((height, D), F32)
-        for p in range(first, last):
-            rows = [spots[4 * p + s : 4 * p + s + 1, :] for s in range(4)]
-            acc = acc + dot(one_hot(rows, height, base), terms[512 * p : 512 * (p + 1), :])
-        return acc
-
-    last = len(CHUNKS) - 1
-    small_steps = [(1, 0), (1, last), (0, 0), (0, last)]
-    big_steps = [(other, c) for c in range(1, last) for other in (1, 0)]
-
-    def early_step(t, carry):
-        early[t] = summed(base_of(t, small_steps), SMALL, 0, 8)
-        return carry
-
-    with jax.named_scope("early"):
-        lax.fori_loop(0, EARLY, early_step, 0)
+    with jax.named_scope("a_sums1a"):
+        a_sums(1, [HALF, HALF + CHUNK], CHUNK)
 
     with jax.named_scope("wait_ag_b"):
         wait_bytes(full_b.at[0, 0:384], sems.at[11])
@@ -492,77 +475,88 @@
         wait_bytes(da_recv.at[1:OWNERS], sems.at[13])
 
     def d_block(j, carry):
-        at = pl.ds(pl.multiple_of(j * 512, 512), 512)
-        rows = da_recv[pl.ds(8 * j, 8)].reshape(512, D).astype(F32)
+        at = pl.ds(pl.multiple_of(j * 1024, 1024), 1024)
+        rows = da_recv[pl.ds(16 * j, 16)].reshape(1024, D).astype(F32)
         for h in range(2):
             both = dot(pick_d[at, :], table_w[h])
             value = (both[:, :LANES] + both[:, LANES:]) * rows[:, h * LANES : (h + 1) * LANES]
-            terms[
-                pl.ds(pl.multiple_of(ROWS + j * 512, 512), 512), h * LANES : (h + 1) * LANES
-            ] = value.astype(BF16)
+            terms[at, h * LANES : (h + 1) * LANES] = value.astype(BF16)
         return carry
 
     with jax.named_scope("d_terms"):
-        lax.fori_loop(0, 4, d_block, 0)
-
-    def finish_step(t, some, held_sum):
-        for n, other, c in some:
-            start, size = CHUNKS[c]
-
-            @pl.when(t == n)
-            def _(other=other, c=c, start=start, size=size):
-                rows = slice(start, start + size)
-                if other:
-                    near_send[rows] = held_sum[...]
-                    send(
-                        near_send.at[rows], near_recv.at[rows], near_sems.at[0, c],
-                        near_sems.at[1, c], {"keys": partner, "view": x},
-                    ).start()
-                    return
-                wait_bytes(near_recv.at[rows], near_sems.at[1, c])
-                acc = held_sum[...] + near_recv[rows]
-                if c == last:
-                    own[...] = acc[size - GROUPS_DEV :, :]
-                blocks = slice(start // GROUPS_DEV, (start + size) // GROUPS_DEV)
-                far_send[blocks] = acc.astype(BF16).reshape(size // GROUPS_DEV, GROUPS_DEV, D)
-                if c == 0:
-                    pl.semaphore_wait(planes, VIEWS - 1)
-                for m in range(blocks.start, blocks.stop):
-                    code = FAR_FIRST[m]
-                    if code:
-                        send(
-                            far_send.at[m], far_recv.at[code], sems.at[22], sems.at[23], peer(code)
-                        ).start()
-
-    def begun_step(t, carry):
-        small_sum[...] = early[t] + summed(base_of(t, small_steps), SMALL, 8, 12)
-        finish_step(t, [(n, *small_steps[n]) for n in range(EARLY)], small_sum)
-        return carry
-
-    def big_step(t, carry):
-        big_sum[...] = summed(base_of(t, big_steps), CHUNK, 0, 12)
-        finish_step(t, [(n, *step) for n, step in enumerate(big_steps)], big_sum)
-        return carry
-
-    def last_step(t, carry):
-        small_sum[...] = summed(base_of(t, small_steps), SMALL, 0, 12)
-        finish_step(t, [(n, *small_steps[n]) for n in range(EARLY, 4)], small_sum)
-        return carry
-
-    with jax.named_scope("begun"):
-        lax.fori_loop(0, EARLY, begun_step, 0)
-    with jax.named_scope("groups"):
-        lax.fori_loop(0, len(big_steps), big_step, 0)
-    with jax.named_scope("last"):
-        lax.fori_loop(EARLY, 4, last_step, 0)
-
-    with jax.named_scope("wait_far"):
-        wait_bytes(far_recv.at[1:PEERS], sems.at[23])
-    with jax.named_scope("tail"):
-        total = own[...]
-        for j in range(1, PEERS):
-            total = total + far_recv[j].astype(F32)
-        out[...] = total
+        lax.fori_loop(0, 2, d_block, 0)
+
+    def to_partner(c):
+        rows = slice(c * CHUNK, (c + 1) * CHUNK)
+        near_send[rows] = chunk_sum[...]
+        send(
+            near_send.at[rows], near_recv.at[rows], near_sems.at[0, c], near_sems.at[1, c],
+            {"keys": partner, "view": x},
+        ).start()
+
+    def to_groups(c):
+        rows = slice(c * CHUNK, (c + 1) * CHUNK)
+        blocks = range(c * CHUNK // GROUPS_DEV, (c + 1) * CHUNK // GROUPS_DEV)
+        wait_bytes(near_recv.at[rows], near_sems.at[1, c])
+        acc = chunk_sum[...] + near_recv[rows]
+        if blocks.stop == PEERS:
+            own[...] = acc[CHUNK - GROUPS_DEV :, :]
+        far_send[blocks.start : blocks.stop] = acc.astype(BF16).reshape(
+            len(blocks), GROUPS_DEV, D
+        )
+        if c == 0:
+            pl.semaphore_wait(planes, VIEWS - 1)
+        for m in blocks:
+            code = FAR_FIRST[m]
+            if code:
+                send(
+                    far_send.at[m], far_recv.at[m], sems.at[22], far_sems.at[c], peer(code)
+                ).start()
+
+    def d_sum(base):
+        acc = jnp.zeros((CHUNK, D), F32)
+        for p in range(4):
+            rows = [spots[32 + 4 * p + s : 33 + 4 * p + s, :] for s in range(4)]
+            acc = acc + dot(one_hot(rows, CHUNK, base), terms[512 * p : 512 * (p + 1), :])
+        return acc
+
+    def sums(steps, begun):
+        def block(t, carry):
+            base = pick_base(t, [other * HALF + c * CHUNK for other, c in steps])
+            base = pl.multiple_of(base, CHUNK)
+            at = pl.ds(base, CHUNK)
+            if begun:
+                chunk_sum[...] = d_sum(base) + part_sum[at, :]
+            else:
+                turned = a_sum(1, base, CHUNK)
+                acc = d_sum(base)
+                chunk_sum[:, :LANES] = acc[:, :LANES] + part_sum[at, :LANES]
+                chunk_sum[:, LANES:] = acc[:, LANES:] + turned
+            for n, (other, c) in enumerate(steps):
+                pl.when(t == n)(lambda other=other, c=c: (to_partner if other else to_groups)(c))
+            return carry
+
+        lax.fori_loop(0, len(steps), block, 0)
+
+    with jax.named_scope("sums1"):
+        sums([(1, 0), (1, 1)], True)
+    with jax.named_scope("sums2"):
+        sums([(0, 0), (0, 1)], False)
+    with jax.named_scope("sums3"):
+        a_sums(0, [HALF + 1024])
+        sums([(1, 2), (1, 3)], False)
+    with jax.named_scope("sums4"):
+        a_sums(0, [1024])
+        sums([(0, 2), (0, 3)], False)
+
+    total = own[...]
+    for c in range(HALF // CHUNK):
+        first, stop = c * CHUNK // GROUPS_DEV, min((c + 1) * CHUNK // GROUPS_DEV, PEERS - 1)
+        with jax.named_scope("wait_far" if stop == PEERS - 1 else "arrive"):
+            wait_bytes(far_recv.at[first:stop], far_sems.at[c])
+        for m in range(first, stop):
+            total = total + far_recv[m].astype(F32)
+    out[...] = total
 
     wait_bytes(db_info.at[1:OWNERS], sems.at[0])
     wait_bytes(db_send.at[0, 1:OWNERS], sems.at[2])
@@ -577,8 +571,8 @@
         wait_bytes(got_db.at[1, :, 0:64], part_sems.at[h, 0])
     wait_bytes(part_db.at[0, 0:384], sems.at[14])
     wait_bytes(far_send.at[0 : PEERS - 1], sems.at[22])
-    for c, (start, size) in enumerate(CHUNKS):
-        wait_bytes(near_send.at[start : start + size], near_sems.at[0, c])
+    for c in range(HALF // CHUNK):
+        wait_bytes(near_send.at[c * CHUNK : (c + 1) * CHUNK], near_sems.at[0, c])
 
 
 def shards(
@@ -635,11 +629,11 @@
             held(2, 128, LANES),
             held(2, 3, 128, LANES),
             held(2, KEYS_DEV, LANES),
-            held(ROWS, KEYS_DEV, dtype=BF16),
+            held(KEYS_DEV, ROWS, dtype=BF16),
             held(OWNERS * CAP, KEYS_DEV, dtype=BF16),
+            held(D, KEYS_DEV, dtype=BF16),
             held(2, KEYS_DEV, D, dtype=BF16),
-            held(2, KEYS_DEV, D, dtype=BF16),
-            held(ROWS + OWNERS * CAP, D, dtype=BF16),
+            held(OWNERS * CAP, D, dtype=BF16),
             held(48, LANES, dtype=I32),
             held(HALF, D),
             held(HALF, D),
@@ -647,12 +641,15 @@
             held(PEERS, GROUPS_DEV, D, dtype=BF16),
             held(GROUPS_DEV, D),
             held(CHUNK, D),
-            held(SMALL, D),
-            held(EARLY, SMALL, D),
+            held(PEERS * 2 * GROUPS_DEV, D),
+            held(ROWS, LANES, dtype=I32),
+            held(2, LANES, ROWS, dtype=BF16),
+            held(2, LANES, ROWS, dtype=BF16),
             pltpu.SemaphoreType.DMA((17,)),
             pltpu.SemaphoreType.DMA((26,)),
-            pltpu.SemaphoreType.DMA((2, len(CHUNKS))),
+            pltpu.SemaphoreType.DMA((2, HALF // CHUNK)),
             pltpu.SemaphoreType.DMA((2, 2)),
+            pltpu.SemaphoreType.DMA((HALF // CHUNK,)),
             pltpu.SemaphoreType.REGULAR,
         ],
         compiler_params=pltpu.CompilerParams(

time: 65.9 us -> 64.8 us (0.983)
  Pallas kernels: 63 us -> 61.9 us
    pallas_call x1, Pallas kernels: 63 us -> 61.9 us  [shards(): pl.pallas_call(kernel, out_shape=jax.ShapeDtypeStruct((GROUPS_DEV, D), F3...]
where the time goes in v5:
time: 64.8 us; the launch traced here: 64.5 us
  Pallas kernels  61.9 us (96%)
  local copies, waits for them, and re-layouts  1.38 us (2%)
  between operations  1.31 us (2%)
    pallas_call x1, Pallas kernels, shards(): pl.pallas_call(kernel, out_shape=jax.ShapeDtypeStruct((GROUPS_DEV, D), F3...  61.9 us
    unnamed x1, local copies, waits for them, and re-layouts  1.38 us

profile of v5, /device:TPU:1, one launch (start us, length us, event | category | flops | bytes accessed | tf_op | source)
XLA Modules:
  0.0 64.5 jit_solution(2373960188120100604)
XLA Ops:
  1.3 61.9 %shard_map.163 = f32[32,256]{1,0:T(8,128)} custom-call(s32[128,128]{1,0:T(8,128)} %bitcast.11, s32[8,128]{1,0:T(8,128)} %bitcast.17, s32[8,128]{1,0:T(8,128)} %bitcast.18, s32[1]{0:T(128)S(6)} %copy.20.db_count_hbm, bf16[1024,256]{1,0:T(8,128)(2,1)} %db_hbm.1, s32[32,128]{1,0:T(8,128)} %bitcast.12, s32[32,128]{1,0:T(8,128)} %bitcast.13, ...), custom_call_target="tpu_custom_call" | custom-call | tf_op jit(solution)/shard_map/pallas_call | solution.py:591
  63.2 1.4 %copy.21 = f32[32,256]{1,0:T(8,128)} copy(f32[32,256]{1,0:T(8,128)} %shard_map.163) | data formatting | bytes 65536

commit v6 on v5

--- a/solution.py
+++ b/solution.py
@@ -463,7 +463,7 @@
     with jax.named_scope("a_terms1"):
         a_terms(1)
     with jax.named_scope("a_sums1a"):
-        a_sums(1, [HALF, HALF + CHUNK], CHUNK)
+        a_sums(1, [HALF])
 
     with jax.named_scope("wait_ag_b"):
         wait_bytes(full_b.at[0, 0:384], sems.at[11])

time: 64.8 us -> 64.7 us (level)
  no operation moved by 1% of the time
where the time goes in v6:
time: 64.7 us; the launch traced here: 64.5 us
  Pallas kernels  61.8 us (96%)
  local copies, waits for them, and re-layouts  1.38 us (2%)
  between operations  1.31 us (2%)
    pallas_call x1, Pallas kernels, shards(): pl.pallas_call(kernel, out_shape=jax.ShapeDtypeStruct((GROUPS_DEV, D), F3...  61.8 us
    unnamed x1, local copies, waits for them, and re-layouts  1.38 us

profile of v6, /device:TPU:1, one launch (start us, length us, event | category | flops | bytes accessed | tf_op | source)
XLA Modules:
  0.0 64.5 jit_solution(11647988649050896799)
XLA Ops:
  1.3 61.8 %shard_map.163 = f32[32,256]{1,0:T(8,128)} custom-call(s32[128,128]{1,0:T(8,128)} %bitcast.11, s32[8,128]{1,0:T(8,128)} %bitcast.17, s32[8,128]{1,0:T(8,128)} %bitcast.18, s32[1]{0:T(128)S(6)} %copy.20.db_count_hbm, bf16[1024,256]{1,0:T(8,128)(2,1)} %db_hbm.1, s32[32,128]{1,0:T(8,128)} %bitcast.12, s32[32,128]{1,0:T(8,128)} %bitcast.13, ...), custom_call_target="tpu_custom_call" | custom-call | tf_op jit(solution)/shard_map/pallas_call | solution.py:591
  63.1 1.4 %copy.21 = f32[32,256]{1,0:T(8,128)} copy(f32[32,256]{1,0:T(8,128)} %shard_map.163) | data formatting | bytes 65536
